TPU v7x, 32 devices: a whole 2x2x4 slice. The times are simulated.
32 devices in a mesh: sta: 16 (over z, x, core), tm: 2 (over y).
Axes of the slice: x: 2, y: 2, z: 4, core: 2. Of those that a mesh axis runs over, the one named last changes fastest.
Arguments:
- records: bfloat16 [32, 3, 1024], P('sta', None, 'tm'), may hold values from -6 to 6
- templates: bfloat16 [512, 32, 3, 150], P(None, 'sta'), may hold values from -6 to 6
- moveout: int32 [512, 32], P(None, 'sta'), may hold values from 0 to 256
- gap_start: int32 [32, 3], P('sta'), may hold values from 0 to 1023
- gap_length: int32 [32, 3], P('sta'), may hold values from 0 to 599
Outputs:
- detection: float32 [512, 1024], P('sta', 'tm')
Inputs may be any that keep to these rules, and one draw needn't show every extreme that they name: `gap_length`: each channel has one gap, counted in samples of the whole window; it may run past the window's end.
All inputs are finite; a program needn't handle non-finite values.
Results may differ from a plain program's by a relative error of at most 0.0041.
Values may be sent and summed in bfloat16 or wider, within the bound.
No kernel may reach another device: no remote copies, remote signals or barrier semaphores. Data moves between devices by JAX's collectives and lax.ppermute only.
A program may use at most 64 MiB of HBM per device.

v0:
```python
import math

import jax
import jax.numpy as jnp
from jax import lax
from jax.sharding import PartitionSpec as P

CHANNELS = 3
TEMPLATE_LEN = 150
TEMPLATES = 512
MAXMO = 256


def passed_along(value, axis, by):
    devices = lax.axis_size(axis)
    pairs = [(i, i + by) for i in range(devices) if 0 <= i + by < devices]
    return lax.ppermute(value, axis, pairs)


def hankel(extended, full_width):
    return jnp.stack(
        [extended[..., offset : offset + full_width] for offset in range(TEMPLATE_LEN)], axis=-2
    )


def whiten(extended, full_width):
    widened = hankel(extended, full_width).astype(jnp.float32)
    energy = jnp.sum(widened * widened, axis=-2, keepdims=True)
    return (widened / jnp.sqrt(jnp.maximum(energy, 1.0))).astype(jnp.bfloat16)


def unit_templates(templates):
    widened = templates.astype(jnp.float32)
    return (widened / jnp.sqrt(jnp.sum(widened * widened, axis=-1, keepdims=True) + 1e-06)).astype(
        jnp.bfloat16
    )


def gap_mask(positions, gap_start, gap_length):
    first = gap_start[..., None]
    return (positions < first) | (positions >= first + gap_length[..., None])


def shift_rows(correlation, lag_column, slice_len):
    current = correlation
    bound = MAXMO
    for level in reversed(range(MAXMO.bit_length())):
        step_size = 1 << level
        new_width = slice_len + min(step_size - 1, bound)
        moved = current[:, step_size:]
        if moved.shape[1] < new_width:
            moved = jnp.pad(moved, ((0, 0), (0, new_width - moved.shape[1])))
        else:
            pass
        kept = current[:, :new_width]
        flagged = (lag_column // step_size % 2 == 1)[:, None]
        current = jnp.where(flagged, moved, kept)
        bound = min(step_size - 1, bound)
    return current


def shards(records, templates, moveout, gap_start, gap_length):
    sta_dev = records.shape[0]
    slice_len = records.shape[2]
    halo_width = MAXMO + TEMPLATE_LEN - 1
    following = passed_along(records[:, :, :halo_width], "tm", -1)
    extended = jnp.concatenate([records, following], axis=2)
    positions = lax.axis_index("tm") * slice_len + jnp.arange(
        slice_len + halo_width, dtype=jnp.int32
    )
    kept_mask = gap_mask(positions, gap_start, gap_length)
    extended = jnp.where(kept_mask, extended, jnp.zeros_like(extended))
    full_width = slice_len + MAXMO
    lagged = whiten(extended, full_width).reshape(sta_dev, CHANNELS * TEMPLATE_LEN, full_width)
    normed = unit_templates(templates).reshape(TEMPLATES, sta_dev, CHANNELS * TEMPLATE_LEN)

    def add_station(station, running):
        weight_rows = lax.dynamic_index_in_dim(normed, station, 1, keepdims=False)
        station_data = lax.dynamic_index_in_dim(lagged, station, 0, keepdims=False)
        correlation = jnp.dot(weight_rows, station_data, preferred_element_type=jnp.float32)
        lag_column = lax.dynamic_index_in_dim(moveout, station, 1, keepdims=False)
        return running + shift_rows(correlation, lag_column, slice_len)

    stacked = lax.psum_scatter(
        lax.fori_loop(0, sta_dev, add_station, jnp.zeros((TEMPLATES, slice_len), jnp.float32)),
        "sta",
        scatter_dimension=0,
        tiled=True,
    )
    stations_all = sta_dev * lax.axis_size("sta")
    return stacked * math.sqrt(TEMPLATE_LEN / (3.0 * stations_all))


def solution(mesh):
    placed = (
        P("sta", None, "tm"),
        P(None, "sta", None, None),
        P(None, "sta"),
        P("sta", None),
        P("sta", None),
    )
    return jax.shard_map(
        shards, mesh=mesh, in_specs=placed, out_specs=P("sta", "tm"), check_vma=False
    )
```

profile of v0, /device:TPU:0, one launch (start us, length us, event | category | flops | bytes accessed | tf_op | source)
XLA Modules:
  0.0 112.5 jit_solution(2478289512785618225)
XLA Ops:
  6.5 1.4 %collective-permute-start = (bf16[2,3,405]{2,0,1:T(2,128)(2,1)}, bf16[2,3,405]{2,0,1:T(2,128)(2,1)S(1)}, u32[]{:S(2)}, u32[]{:S(2)}) collective-permute-start(bf16[2,3,405]{2,0,1:T(2,128)(2,1)} %bitcast.613), channel_id=1, source_target_pairs={{1,0},{3,2},{5,4},{7,6},{9,8},{11,10},{13,12},{15,14},{17,16},{19,... | collective-permute-start | bytes 14588 | tf_op jit(solution)/shard_map/ppermute | solution.py:17
  8.0 2.1 %fusion.17 = f32[512,2,3]{0,1,2:T(2,128)S(1)} fusion(bf16[512,2,3,150]{0,1,3,2:T(2,128)(2,1)} %param.8), kind=kLoop, calls=%fused_computation.92 | loop fusion | flops 1379328 | bytes 933888 | tf_op jit(solution)/shard_map/reduce_sum | solution.py:34
  10.2 0.7 fusion.18
  11.3 1.5 %collective-permute-done = bf16[2,3,405]{2,0,1:T(2,128)(2,1)S(1)} collective-permute-done((bf16[2,3,405]{2,0,1:T(2,128)(2,1)}, bf16[2,3,405]{2,0,1:T(2,128)(2,1)S(1)}, u32[]{:S(2)}, u32[]{:S(2)}) %collective-permute-start) | collective-permute-done | bytes 4892 | tf_op jit(solution)/shard_map/ppermute | solution.py:17
  26.3 1.5 %fusion.15 = f32[2,3,768]{2,0,1:T(2,128)S(1)} fusion(bf16[2,3,150,768]{3,0,1,2:T(2,128)(2,1)S(1)} %constant_dynamic-update-slice_fusion), kind=kLoop, calls=%fused_computation.88 | loop fusion | flops 2068992 | bytes 1400832 | tf_op jit(solution)/shard_map/reduce_sum | solution.py:28
  27.8 1.1 fusion.16
  28.9 0.2 copy.13
  29.1 1.5 %convert_element_type.30 = bf16[2,450,768]{2,1,0:T(8,128)(2,1)} reshape(bf16[2,3,150,768]{3,2,1,0:T(8,128)(2,1)S(1)} %copy.13) | data formatting | bytes 2764800 | tf_op jit(solution)/shard_map/convert_element_type | solution.py:29
  30.6 12.2 %while.17 = (s32[]{:T(128)}, f32[512,512]{1,0:T(8,128)S(1)}, s32[512,2]{0,1:T(2,128)S(1)}, bf16[512,2,450]{0,2,1:T(8,128)(2,1)S(1)}, bf16[2,450,768]{2,1,0:T(8,128)(2,1)}, /*index=5*/s32[]{:T(128)}, s32[]{:T(128)}) while((s32[]{:T(128)}, f32[512,512]{1,0:T(8,128)S(1)}, s32[512,2]{0,1:T(2,128)S(1)}, ...), condition=%wide.region_3.4_spmd.clone, body=%wide.region_2.3_spmd.clone.sunk | while | flops 357130240 | bytes 36771928 | solution.py:85
  30.6 0.2 compare_reduce_fusion.10
  30.7 1.7 %fusion.25 = f32[512,768]{1,0:T(8,128)S(1)} fusion(bf16[2,450,768]{2,1,0:T(8,128)(2,1)} %get-tuple-element.290, s32[]{:T(128)} %get-tuple-element.279, bf16[512,2,450]{0,2,1:T(8,128)(2,1)S(1)} %get-tuple-element.289), kind=kOutput, calls=%fused_computation.10.clone.1 | convolution fusion | flops 353894400 | bytes 2741248 | tf_op jit(solution)/shard_map/while/body/eval_jaxpr/dot_general | solution.py:80
  32.6 0.2 slice_select_fusion.17
  33.0 0.5 slice_select_fusion.19
  33.5 0.5 slice_select_fusion.20
  34.0 0.5 slice_select_fusion.21
  34.5 0.5 slice_select_fusion.22
  35.0 0.5 slice_select_fusion.23
  35.5 0.5 slice_select_fusion.24
  36.0 0.7 fusion.26
  36.7 0.2 compare_reduce_fusion.10
  36.9 1.7 %fusion.25 = f32[512,768]{1,0:T(8,128)S(1)} fusion(bf16[2,450,768]{2,1,0:T(8,128)(2,1)} %get-tuple-element.290, s32[]{:T(128)} %get-tuple-element.279, bf16[512,2,450]{0,2,1:T(8,128)(2,1)S(1)} %get-tuple-element.289), kind=kOutput, calls=%fused_computation.10.clone.1 | convolution fusion | flops 353894400 | bytes 2741248 | tf_op jit(solution)/shard_map/while/body/eval_jaxpr/dot_general | solution.py:80
  38.7 0.2 slice_select_fusion.17
  39.1 0.5 slice_select_fusion.19
  39.6 0.5 slice_select_fusion.20
  40.1 0.5 slice_select_fusion.21
  40.6 0.5 slice_select_fusion.22
  41.1 0.5 slice_select_fusion.23
  41.6 0.5 slice_select_fusion.24
  42.1 0.7 fusion.26
  42.8 1.0 copy-done
  43.8 60.4 %reduce-scatter.2.cloned.1.call-done = f32[32,512]{1,0:T(8,128)} async-done(((f32[512,512]{1,0:T(8,128)}), f32[32,512]{1,0:T(8,128)}) %reduce-scatter.2.cloned.1.call-update) | async-done | bytes 65552 | tf_op jit(solution)/shard_map/reduce_scatter | solution.py:84
  104.2 1.5 %broadcast_multiply_fusion = f32[32,512]{1,0:T(8,128)} fusion(f32[32,512]{1,0:T(8,128)} %reduce-scatter.2.cloned.1.call-done), kind=kLoop, calls=%fused_computation.245 | loop fusion | flops 16384 | bytes 131072 | tf_op jit(solution)/shard_map/mul | solution.py:91
  (176 shorter events, 14.1 us)
Async XLA Ops:
  6.5 3.6 %copy-start.1 = (bf16[512,2,3,150]{0,1,3,2:T(2,128)(2,1)S(1)}, bf16[512,2,3,150]{0,1,3,2:T(2,128)(2,1)}, u32[]{:S(2)}) copy-start(bf16[512,2,3,150]{0,1,3,2:T(2,128)(2,1)} %param.8) | copy-start | bytes 2764804
  6.5 97.7 %reduce-scatter.2.cloned.1.call-start = ((), (), s32[]{:S(2)}) async-start(), calls=%async_computation.1 | async-start | bytes 1114112 | tf_op jit(solution)/shard_map/reduce_scatter | solution.py:84
  6.5 6.2 %collective-permute-start = (bf16[2,3,405]{2,0,1:T(2,128)(2,1)}, bf16[2,3,405]{2,0,1:T(2,128)(2,1)S(1)}, u32[]{:S(2)}, u32[]{:S(2)}) collective-permute-start(bf16[2,3,405]{2,0,1:T(2,128)(2,1)} %bitcast.613), channel_id=1, source_target_pairs={{1,0},{3,2},{5,4},{7,6},{9,8},{11,10},{13,12},{15,14},{17,16},{19,... | collective-permute-start | bytes 14588 | tf_op jit(solution)/shard_map/ppermute | solution.py:17
  8.0 3.0 %copy-start.4 = (s32[2,3]{1,0:T(2,128)S(1)}, s32[2,3]{1,0:T(2,128)}, u32[]{:S(2)}) copy-start(s32[2,3]{1,0:T(2,128)} %param.10) | copy-start | bytes 76
  8.0 3.1 %copy-start.5 = (s32[2,3]{1,0:T(2,128)S(1)}, s32[2,3]{1,0:T(2,128)}, u32[]{:S(2)}) copy-start(s32[2,3]{1,0:T(2,128)} %param.11) | copy-start | bytes 76
  10.9 1.9 %copy-start.3 = (bf16[2,3,512]{2,0,1:T(2,128)(2,1)S(1)}, bf16[2,3,512]{2,0,1:T(2,128)(2,1)}, u32[]{:S(2)}) copy-start(bf16[2,3,512]{2,0,1:T(2,128)(2,1)} %param.7) | copy-start | bytes 18436
  29.1 1.5 %copy-start.2 = (s32[512,2]{0,1:T(2,128)S(1)}, s32[512,2]{0,1:T(2,128)}, u32[]{:S(2)}) copy-start(s32[512,2]{0,1:T(2,128)} %param.9) | copy-start | bytes 12292
  42.8 1.0 copy-start
Sparse Core Ops, SparseCore 0:
  44.0 60.2 reduce-scatter.1
where the time goes:
time: 113 us
  waiting for transfers between devices  61.9 us (55%)
  local copies, waits for them, and re-layouts  16.3 us (14%)
  other arithmetic  15.4 us (14%)
  between operations  13.9 us (12%)
  matrix products  3.41 us (3%)
  starting transfers between devices  1.41 us (1%)
    reduce_scatter x1, waiting for transfers between devices, shards(): lax.psum_scatter(lax.fori_loop(0, sta_dev, add_station, jnp.zeros((TEMPLA...  60.4 us
    unnamed x162, local copies, waits for them, and re-layouts  14 us
    select_n x16, other arithmetic, shift_rows(): current = jnp.where(flagged, moved, kept)  6.7 us
    dot_general x2, matrix products, add_station(): jnp.dot(weight_rows, station_data, preferred_element_type=jnp.float32)  3.41 us
  transfers between devices with their start and end apart: 2, of which 2 were waited for; matrix products, arithmetic and copies ran while one was open for 3% of the time, Pallas kernels for 0%

commit v1 on v0

v1 whole, which is shorter than its diff:
```python
import functools
import math

import jax
import jax.numpy as jnp
from jax import lax
from jax.experimental import pallas as pl
from jax.experimental.pallas import tpu as pltpu
from jax.sharding import PartitionSpec as P

CHANNELS = 3
TEMPLATE_LEN = 150
MAXMO = 256
LANES = 128
PADDED = -(-TEMPLATE_LEN // 16) * 16

f32, bf16, i32 = jnp.float32, jnp.bfloat16, jnp.int32


def unit_kernel(raw, unit, apart):
    stations = raw.shape[2]
    for c in range(CHANNELS):
        for j in range(raw.shape[3] // LANES):
            lanes = pl.ds(j * LANES, LANES)
            apart[j] = raw[c, :, :, lanes].astype(f32).reshape(TEMPLATE_LEN * stations, LANES)
            for s in range(stations):
                wave = apart[j, pl.ds(s, TEMPLATE_LEN, stride=stations), :]
                norm = lax.rsqrt(jnp.sum(wave * wave, axis=0, keepdims=True) + 1e-6)
                unit[s, pl.ds(c * PADDED, TEMPLATE_LEN), lanes] = (wave * norm).astype(bf16)
                unit[s, pl.ds(c * PADDED + TEMPLATE_LEN, PADDED - TEMPLATE_LEN), lanes] = jnp.zeros(
                    (PADDED - TEMPLATE_LEN, LANES), bf16
                )


def left(rows, by):
    return rows if by == 0 else pltpu.roll(rows, rows.shape[1] - by, 1)


def mask_and_energy(own, following, first_sample, gap_start, gap_length, rows, staggered, inverse):
    width = own.shape[2]
    stations = own.shape[1]
    full = inverse.shape[1]
    for c in range(CHANNELS):
        at = pl.ds(c * stations, stations)
        rows[at, pl.ds(0, width)] = own[c].astype(f32)
        rows[at, pl.ds(width, width)] = following[c].astype(f32)
    count = rows.shape[0]
    row = lax.broadcasted_iota(i32, (count, 1), 0)
    first = jnp.zeros((count, 1), i32)
    length = jnp.zeros((count, 1), i32)
    for c in range(CHANNELS):
        for s in range(stations):
            here = row == c * stations + s
            first = jnp.where(here, gap_start[s, c], first)
            length = jnp.where(here, gap_length[s, c], length)
    position = first_sample[0] + lax.broadcasted_iota(i32, (count, 2 * width), 1)
    kept = (position < first) | (position >= first + length)
    masked = jnp.where(kept, rows[...], 0.0)
    power, energy, offset, span = masked * masked, None, 0, 1
    while span <= TEMPLATE_LEN:
        if TEMPLATE_LEN & span:
            term = left(power, offset)
            energy = term if energy is None else energy + term
            offset += span
        power = power + left(power, span)
        span *= 2
    inverse[...] = lax.rsqrt(jnp.maximum(energy[:, :full], 1.0))
    for r in range(8):
        moved = left(masked, r)
        for j in range(staggered.shape[0]):
            staggered[j, pl.ds(r, count, stride=8), :] = moved[:, j * LANES : (j + 1) * LANES]


def lag_matrix(staggered, inverse, lagged):
    stations, _, full = lagged.shape
    for s in range(stations):
        for c in range(CHANNELS):
            r = c * stations + s
            eight = jnp.concatenate(
                [staggered[j, pl.ds(8 * r, 8), :] for j in range(staggered.shape[0])], axis=1
            )
            scale = jnp.broadcast_to(inverse[pl.ds(r, 1), :], (8, full))
            for q in range(0, PADDED, 16):
                upper = eight[:, q : q + full] * scale
                lower = eight[:, q + 8 : q + 8 + full] * scale
                lagged[s, pl.ds(c * PADDED + q, 16), :] = jnp.concatenate(
                    [upper, lower], axis=0
                ).astype(bf16)


def shifted(correlation, lags, s, start, count, width):
    tiles = width // LANES
    at = pl.ds(start, count)
    v = [correlation[s, at, pl.ds(j * LANES, LANES)] for j in range(tiles + MAXMO // LANES)]
    lag = jnp.broadcast_to(lags[at, s : s + 1], (count, LANES))
    none, one = lag < LANES, lag < 2 * LANES
    reach = lax.broadcasted_iota(i32, (count, LANES), 1) + lax.rem(lag, LANES)
    within = reach < LANES
    lane = lax.rem(reach, LANES)
    whole = [
        jnp.where(none, v[j], jnp.where(one, v[j + 1], v[min(j + 2, tiles + 1)]))
        for j in range(tiles + 1)
    ]
    fine = [jnp.take_along_axis(t, lane, axis=1, mode="promise_in_bounds") for t in whole]
    return [jnp.where(within, fine[j], fine[j + 1]) for j in range(tiles)]


def stack_kernel(
    own, following, first_sample, gap_start, gap_length, moveout, unit, stack,
    rows, staggered, inverse, lagged, lag_rows, lags, correlation,
):
    stations, templates = moveout.shape
    width = own.shape[2]
    mask_and_energy(own, following, first_sample, gap_start, gap_length, rows, staggered, inverse)
    lag_matrix(staggered, inverse, lagged)
    lag_rows[pl.ds(0, stations), :] = moveout[...].astype(f32)
    for k in range(0, templates, LANES):
        lags[pl.ds(k, LANES), :] = lag_rows[:, pl.ds(k, LANES)].T.astype(i32)
    for s in range(stations):
        correlation[s] = lax.dot_general(
            unit[s], lagged[s], (((0,), (0,)), ((), ())), preferred_element_type=f32
        )
    count = 16

    def block(i, _):
        start = pl.multiple_of(i * count, count)
        total = shifted(correlation, lags, 0, start, count, width)
        for s in range(1, stations):
            total = [a + b for a, b in zip(total, shifted(correlation, lags, s, start, count, width))]
        stack[pl.ds(start, count), :] = jnp.concatenate(total, axis=1).astype(bf16)
        return 0

    lax.fori_loop(0, templates // count, block, 0, unroll=4)


def shards(records, templates, moveout, gap_start, gap_length):
    stations, _, width = records.shape
    number = templates.shape[0]
    full = width + MAXMO
    devices = lax.axis_size("tm")
    own = records.transpose(1, 0, 2)
    following = lax.ppermute(own, "tm", [(i, i - 1) for i in range(1, devices)])
    vmem = pl.BlockSpec(memory_space=pltpu.VMEM)
    smem = pl.BlockSpec(memory_space=pltpu.SMEM)
    params = pltpu.CompilerParams(vmem_limit_bytes=48 * 1024 * 1024)
    depth = CHANNELS * PADDED
    unit = pl.pallas_call(
        unit_kernel,
        out_shape=jax.ShapeDtypeStruct((stations, depth, number), bf16),
        in_specs=[vmem],
        out_specs=vmem,
        scratch_shapes=[pltpu.VMEM((number // LANES, TEMPLATE_LEN * stations, LANES), f32)],
        compiler_params=params,
        cost_estimate=pl.CostEstimate(flops=10**9, bytes_accessed=2 * 10**6, transcendentals=0),
    )(templates.transpose(2, 3, 1, 0))
    first_sample = (lax.axis_index("tm") * width).astype(i32).reshape(1)
    stack = pl.pallas_call(
        stack_kernel,
        out_shape=jax.ShapeDtypeStruct((number, width), bf16),
        in_specs=[vmem, vmem, smem, smem, smem, vmem, vmem],
        out_specs=vmem,
        scratch_shapes=[
            pltpu.VMEM((8, 2 * width), f32),
            pltpu.VMEM((2 * width // LANES, 64, LANES), f32),
            pltpu.VMEM((8, full), f32),
            pltpu.VMEM((stations, depth, full), bf16),
            pltpu.VMEM((8, number), f32),
            pltpu.VMEM((number, 8), i32),
            pltpu.VMEM((stations, number, full), f32),
        ],
        compiler_params=params,
        cost_estimate=pl.CostEstimate(flops=2 * 10**9, bytes_accessed=2 * 10**6, transcendentals=0),
    )(own, following, first_sample, gap_start, gap_length, moveout.T, unit)
    groups = lax.axis_size("sta")
    parts = lax.all_to_all(stack, "sta", 0, 0, tiled=True).reshape(groups, number // groups, width)
    return jnp.sum(parts.astype(f32), axis=0) * math.sqrt(TEMPLATE_LEN / (3.0 * stations * groups))


def solution(mesh):
    placed = (
        P("sta", None, "tm"),
        P(None, "sta", None, None),
        P(None, "sta"),
        P("sta", None),
        P("sta", None),
    )
    return jax.shard_map(
        shards, mesh=mesh, in_specs=placed, out_specs=P("sta", "tm"), check_vma=False
    )
```

time: 113 us -> 35.7 us (0.32)
  waiting for transfers between devices: 61.9 us -> 2.34 us
  blocking collectives: 0 us -> 21.1 us
  other arithmetic: 15.4 us -> 0.71 us
  local copies, waits for them, and re-layouts: 16.3 us -> 1.86 us
  between operations: 13.9 us -> 0.06 us
  Pallas kernels: 0 us -> 8.18 us
  matrix products: 3.41 us -> 0 us
    reduce_scatter x1 -> x0, waiting for transfers between devices: 60.4 us -> none  [shards(): lax.psum_scatter(lax.fori_loop(0, sta_dev, add_station, jnp.zeros((TEMPLA...]
    all_to_all x0 -> x1, blocking collectives: none -> 21.1 us  [shards(): lax.all_to_all(stack, 'sta', 0, 0, tiled=True)]
    unnamed x162 -> x10, local copies, waits for them, and re-layouts: 14 us -> 1.86 us
    pallas_call x0 -> x2, Pallas kernels: none -> 8.18 us  [the longest x1 6.94 us: shards(): pl.pallas_call(stack_kernel, out_shape=jax.ShapeDtypeStruct((number, widt...]
    select_n x17 -> x0, other arithmetic: 6.79 us -> none  [the longest x16 6.7 us: shift_rows(): current = jnp.where(flagged, moved, kept)]
    reduce_sum x2 -> x1, other arithmetic: 3.64 us -> 0.08 us  [shards(): jnp.sum(parts.astype(f32), axis=0)]
    dot_general x2 -> x0, matrix products: 3.41 us -> none  [add_station(): jnp.dot(weight_rows, station_data, preferred_element_type=jnp.float32)]
    convert_element_type x2 -> x0, other arithmetic: 1.81 us -> none  [the longest x1 1.09 us: whiten(): return (widened / jnp.sqrt(jnp.maximum(energy, 1.0))).astype(jnp.bfloat16)]
  transfers between devices with their start and end apart: 2 -> 1, of which waited for: 2 -> 1; matrix products, arithmetic and copies ran while one was open for 3% -> 0% of each run, Pallas kernels for 0% -> 3%
where the time goes in v1:
time: 35.7 us; the launch traced here: 35.5 us
  blocking collectives  21.1 us (59%)
  Pallas kernels  8.18 us (23%)
  waiting for transfers between devices  2.34 us (7%)
  local copies, waits for them, and re-layouts  1.86 us (5%)
  starting transfers between devices  1.28 us (4%)
  other arithmetic  0.71 us (2%)
    all_to_all x1, blocking collectives, shards(): lax.all_to_all(stack, 'sta', 0, 0, tiled=True)  21.1 us
    pallas_call x1, Pallas kernels, shards(): pl.pallas_call(stack_kernel, out_shape=jax.ShapeDtypeStruct((number, widt...  6.94 us
    ppermute x1, waiting for transfers between devices, shards(): following = lax.ppermute(own, 'tm', [(i, i - 1) for i in range(1, devices)])  2.34 us
    unnamed x10, local copies, waits for them, and re-layouts  1.86 us
    ppermute x1, starting transfers between devices, shards(): following = lax.ppermute(own, 'tm', [(i, i - 1) for i in range(1, devices)])  1.28 us
    pallas_call x1, Pallas kernels, shards(): pl.pallas_call(unit_kernel, out_shape=jax.ShapeDtypeStruct((stations, dep...  1.24 us
  transfers between devices with their start and end apart: 1, of which 1 were waited for; matrix products, arithmetic and copies ran while one was open for 0% of the time, Pallas kernels for 3%

profile of v1, /device:TPU:0, one launch (start us, length us, event | category | flops | bytes accessed | tf_op | source)
XLA Modules:
  0.0 35.5 jit_solution(11584041332015533241)
XLA Ops:
  0.0 1.3 %collective-permute-start = (bf16[3,2,512]{2,1,0:T(2,128)(2,1)}, bf16[3,2,512]{2,1,0:T(2,128)(2,1)S(1)}, u32[]{:S(2)}, u32[]{:S(2)}) collective-permute-start(bf16[3,2,512]{2,1,0:T(2,128)(2,1)} %bitcast.7), channel_id=1, source_target_pairs={{1,0},{3,2},{5,4},{7,6},{9,8},{11,10},{13,12},{15,14},{17,16},{19,... | collective-permute-start | bytes 18440 | tf_op jit(solution)/shard_map/ppermute | solution.py:142
  1.3 0.0 copy-start
  1.3 1.2 %copy-done = bf16[512,2,3,150]{0,1,3,2:T(2,128)(2,1)S(1)} copy-done((bf16[512,2,3,150]{0,1,3,2:T(2,128)(2,1)S(1)}, bf16[512,2,3,150]{0,1,3,2:T(2,128)(2,1)}, u32[]{:S(2)}) %copy-start) | copy-done | bytes 921624
  2.5 0.0 copy-start.4
  2.5 1.2 %shard_map.55.unit = bf16[2,480,512]{2,1,0:T(8,128)(2,1)S(1)} custom-call(bf16[3,150,2,512]{3,2,1,0:T(2,128)(2,1)S(1)} %bitcast.6), custom_call_target="tpu_custom_call" | custom-call | flops 1000000000 | bytes 2000000 | tf_op jit(solution)/shard_map/pallas_call | solution.py:147
  3.7 0.0 copy-start.1
  3.7 0.0 copy-start.2
  3.7 2.3 %collective-permute-done.following = bf16[3,2,512]{2,1,0:T(2,128)(2,1)S(1)} collective-permute-done((bf16[3,2,512]{2,1,0:T(2,128)(2,1)}, bf16[3,2,512]{2,1,0:T(2,128)(2,1)S(1)}, u32[]{:S(2)}, u32[]{:S(2)}) %collective-permute-start) | collective-permute-done | bytes 6176 | tf_op jit(solution)/shard_map/ppermute | solution.py:142
  6.1 0.0 copy-start.3
  6.1 0.0 copy-done.4
  6.1 0.0 copy-done.1
  6.1 0.0 copy-done.2
  6.1 0.7 %copy-done.3 = s32[2,3]{1,0:T(2,128)S(1)} copy-done((s32[2,3]{1,0:T(2,128)S(1)}, s32[2,3]{1,0:T(2,128)}, u32[]{:S(2)}) %copy-start.3) | copy-done | bytes 48
  6.8 6.9 %shard_map.56 = bf16[512,512]{1,0:T(8,128)(2,1)S(1)} custom-call(bf16[3,2,512]{2,1,0:T(2,128)(2,1)S(1)} %bitcast.8, bf16[3,2,512]{2,1,0:T(2,128)(2,1)S(1)} %collective-permute-done.following, s32[1]{0:T(128)} %bitcast.1.first_sample, s32[2,3]{1,0:T(2,128)S(1)} %copy-done.3, s32[2,3]{1,0:T(2,128)S(1)} %copy-done.4, s32[2,512]{1,0:T(2,128)S(1)} %bitcast.9, ...), custom_call_target="tpu_custom_call" | custom-call | flops 2000000000 | bytes 2000000 | tf_op jit(solution)/shard_map/pallas_call | solution.py:157
  13.7 21.1 %all_to_all.9 = bf16[16,32,512]{2,1,0:T(8,128)(2,1)S(1)} all-to-all(bf16[16,32,512]{2,1,0:T(8,128)(2,1)S(1)} %bitcast.5), channel_id=1, replica_groups=mesh['sta'=16,'tm'=2] {'sta'}, dimensions={0} | all-to-all | bytes 1048576 | tf_op jit(solution)/shard_map/all_to_all | solution.py:175
  34.8 0.1 convert_reduce_fusion
  34.9 0.6 %broadcast_multiply_fusion = f32[32,512]{1,0:T(8,128)} fusion(f32[32,512]{1,0:T(8,128)S(1)} %convert_reduce_fusion), kind=kLoop, calls=%fused_computation.1 | loop fusion | flops 16384 | bytes 131072 | tf_op jit(solution)/shard_map/mul | solution.py:176
Async XLA Ops:
  0.0 6.1 %collective-permute-start = (bf16[3,2,512]{2,1,0:T(2,128)(2,1)}, bf16[3,2,512]{2,1,0:T(2,128)(2,1)S(1)}, u32[]{:S(2)}, u32[]{:S(2)}) collective-permute-start(bf16[3,2,512]{2,1,0:T(2,128)(2,1)} %bitcast.7), channel_id=1, source_target_pairs={{1,0},{3,2},{5,4},{7,6},{9,8},{11,10},{13,12},{15,14},{17,16},{19,... | collective-permute-start | bytes 18440 | tf_op jit(solution)/shard_map/ppermute | solution.py:142
  1.3 1.2 %copy-start = (bf16[512,2,3,150]{0,1,3,2:T(2,128)(2,1)S(1)}, bf16[512,2,3,150]{0,1,3,2:T(2,128)(2,1)}, u32[]{:S(2)}) copy-start(bf16[512,2,3,150]{0,1,3,2:T(2,128)(2,1)} %param.6) | copy-start | bytes 2764804
  2.5 3.6 %copy-start.4 = (s32[2,3]{1,0:T(2,128)S(1)}, s32[2,3]{1,0:T(2,128)}, u32[]{:S(2)}) copy-start(s32[2,3]{1,0:T(2,128)} %gap_length.1) | copy-start | bytes 76
  3.7 2.4 %copy-start.1 = (bf16[2,3,512]{2,0,1:T(2,128)(2,1)S(1)}, bf16[2,3,512]{2,0,1:T(2,128)(2,1)}, u32[]{:S(2)}) copy-start(bf16[2,3,512]{2,0,1:T(2,128)(2,1)} %param.5) | copy-start | bytes 18436
  3.7 2.4 %copy-start.2 = (s32[512,2]{0,1:T(2,128)S(1)}, s32[512,2]{0,1:T(2,128)}, u32[]{:S(2)}) copy-start(s32[512,2]{0,1:T(2,128)} %param.7) | copy-start | bytes 12292
  6.1 0.7 %copy-start.3 = (s32[2,3]{1,0:T(2,128)S(1)}, s32[2,3]{1,0:T(2,128)}, u32[]{:S(2)}) copy-start(s32[2,3]{1,0:T(2,128)} %gap_start.1) | copy-start | bytes 76

commit v2 on v0

v2 whole, which is shorter than its diff:
```python
import functools
import math

import jax
import jax.numpy as jnp
from jax import lax
from jax.experimental import pallas as pl
from jax.experimental.pallas import tpu as pltpu
from jax.sharding import PartitionSpec as P

CHANNELS = 3
TEMPLATE_LEN = 150
MAXMO = 256
FACTORS = (5, 5, 3, 2)
LANES = 128
PADDED = -(-TEMPLATE_LEN // 16) * 16

STEP = 16

f32, bf16, i32 = jnp.float32, jnp.bfloat16, jnp.int32


def setup_kernel(
    raw_hbm, moveout_hbm, gap_start_hbm, gap_length_hbm, own_hbm,
    unit, lags, kept, masked,
    raw, moveout, gap_start, gap_length, own, apart, tall, lag_rows, rows, sems,
):
    stations, templates = moveout.shape
    width = own.shape[2]
    copies = [pltpu.make_async_copy(raw_hbm.at[c], raw.at[c], sems.at[c]) for c in range(CHANNELS)]
    small = [(moveout_hbm, moveout), (gap_start_hbm, gap_start), (gap_length_hbm, gap_length), (own_hbm, own)]
    small = [pltpu.make_async_copy(a, b, sems.at[CHANNELS + i]) for i, (a, b) in enumerate(small)]
    for copy in small + copies:
        copy.start()
    for copy in small:
        copy.wait()
    lag_rows[...] = jnp.zeros_like(lag_rows)
    lag_rows[pl.ds(0, stations), :] = moveout[...].astype(f32)
    for k in range(0, templates, LANES):
        columns = lag_rows[:, pl.ds(k, LANES)].T
        for s in range(stations):
            lags[s, pl.ds(k, LANES), :] = jnp.broadcast_to(columns[:, s : s + 1], (LANES, LANES)).astype(i32)
    count = rows.shape[0]
    row = lax.broadcasted_iota(i32, (count, 1), 0)
    first = jnp.zeros((count, 1), i32)
    length = jnp.zeros((count, 1), i32)
    rows[...] = jnp.zeros_like(rows)
    for c in range(CHANNELS):
        rows[pl.ds(c * stations, stations), :] = own[c].astype(f32)
        for s in range(stations):
            here = row == c * stations + s
            first = jnp.where(here, gap_start[s, c], first)
            length = jnp.where(here, gap_length[s, c], length)
    position = lax.axis_index("tm") * width + lax.broadcasted_iota(i32, (count, 2 * width), 1)
    keep = ((position < first) | (position >= first + length)) & (position < lax.axis_size("tm") * width)
    kept[...] = jnp.where(keep[:, width:], 1.0, 0.0)
    masked[...] = jnp.where(keep[:, :width], rows[...], 0.0)
    tall[...] = jnp.zeros_like(tall)
    groups = templates // LANES
    for c in range(CHANNELS):
        copies[c].wait()
        apart[...] = raw[c].astype(f32)
        for j in range(groups):
            for s in range(stations):
                wave = apart[pl.ds(j * stations + s, TEMPLATE_LEN, stride=groups * stations), :]
                norm = lax.rsqrt(jnp.sum(wave * wave, axis=0, keepdims=True) + 1e-6)
                tall[s, j, pl.ds(c * PADDED, TEMPLATE_LEN), :] = (wave * norm).astype(bf16)
    for s in range(stations):
        for j in range(templates // LANES):
            unit[s, pl.ds(j * LANES, LANES), :] = tall[s, j].T


def left(rows, by):
    return rows if by == 0 else pltpu.roll(rows, rows.shape[1] - by, 1)


def lag_matrix(masked, kept, following, staggered, inverse, lagged):
    stations, _, full = lagged.shape
    count, width = masked.shape
    beyond = [jnp.zeros((count - CHANNELS * stations, width), f32)]
    after = jnp.concatenate([following[c].astype(f32) for c in range(CHANNELS)] + beyond, axis=0)
    samples = jnp.concatenate([masked[...], jnp.where(kept[...] > 0.5, after, 0.0)], axis=1)
    energy, span = samples * samples, 1
    for factor in FACTORS:
        energy = sum((left(energy, i * span) for i in range(1, factor)), energy)
        span *= factor
    inverse[...] = lax.rsqrt(jnp.maximum(energy[:, :full], 1.0))
    for r in range(STEP):
        moved = left(samples, r)
        for j in range(staggered.shape[0]):
            staggered[j, pl.ds(r, count, stride=STEP), :] = moved[:, j * LANES : (j + 1) * LANES]
    lane = lax.broadcasted_iota(i32, (STEP, LANES), 1)
    for s in range(stations):
        for c in range(CHANNELS):
            r = c * stations + s
            tiles = [
                staggered[j, pl.ds(STEP * r, STEP), :].astype(bf16) for j in range(staggered.shape[0])
            ]
            scale = [
                jnp.broadcast_to(inverse[pl.ds(r, 1), pl.ds(j * LANES, LANES)], (STEP, LANES))
                for j in range(full // LANES)
            ]
            for turn in range(0, min(PADDED, LANES), STEP):
                turned = [pltpu.roll(t, LANES - turn, 1) if turn else t for t in tiles]
                near = [
                    jnp.where(lane < LANES - turn, x, y) if turn else x
                    for x, y in zip(turned, turned[1:] + turned[:1])
                ]
                for q in range(turn, PADDED, LANES):
                    for j in range(full // LANES):
                        lagged[s, pl.ds(c * PADDED + q, STEP), pl.ds(j * LANES, LANES)] = (
                            near[j + q // LANES].astype(f32) * scale[j]
                        ).astype(bf16)


def shifted(correlation, lags, s, row, template, count, width):
    tiles = width // LANES
    at = pl.ds(row, count)
    v = [correlation[s, at, pl.ds(j * LANES, LANES)] for j in range(tiles + MAXMO // LANES)]
    lag = lags[s, pl.ds(template, count), :]
    none, one = lag < LANES, lag < 2 * LANES
    reach = lax.broadcasted_iota(i32, (count, LANES), 1) + (lag & (LANES - 1))
    within = reach < LANES
    lane = reach & (LANES - 1)
    whole = [
        jnp.where(none, v[j], jnp.where(one, v[j + 1], v[min(j + 2, tiles + 1)]))
        for j in range(tiles + 1)
    ]
    fine = [jnp.take_along_axis(t, lane, axis=1, mode="promise_in_bounds") for t in whole]
    return [jnp.where(within, fine[j], fine[j + 1]) for j in range(tiles)]


def stack_rows(correlation, lags, first, templates_of, target, scale):
    stations = correlation.shape[0]
    width = target.shape[1]
    count = 16

    def block(i, _):
        to = pl.multiple_of(i * count, count)
        template = pl.multiple_of(templates_of(i), count)
        total = shifted(correlation, lags, 0, first + to, template, count, width)
        for s in range(1, stations):
            more = shifted(correlation, lags, s, first + to, template, count, width)
            total = [a + b for a, b in zip(total, more)]
        for j, t in enumerate(total):
            target[pl.ds(to, count), pl.ds(j * LANES, LANES)] = (t * scale).astype(target.dtype)
        return 0

    lax.fori_loop(0, target.shape[0] // count, block, 0, unroll=8)


def place():
    me = lax.axis_index("sta")
    return me & 1, (me >> 1) & 1, me >> 2


def rows_of(owned, block_of):
    per = owned // 16
    return lambda i: block_of(i // per) * owned + i % per * 16


def correlate(owned, unit, lagged, block_of, correlation):
    for s in range(unit.shape[0]):
        blocks = [
            unit[s, pl.ds(pl.multiple_of(block_of(b) * owned, 16), owned), :]
            for b in range(correlation.shape[1] // owned)
        ]
        correlation[s] = jnp.dot(
            jnp.concatenate(blocks, axis=0), lagged[s], preferred_element_type=f32
        )


def owners(rest, across):
    core, pair, _ = place()
    return lambda b: (b % rest * 2 + (pair ^ across)) * 2 + (core ^ 1 ^ (b // rest))


def first_kernel(
    owned, scale, masked, kept, following, unit, lags, lagged, correlation, away, staggered, inverse,
):
    lag_matrix(masked, kept, following, staggered, inverse, lagged)
    block_of = owners(away.shape[0] // owned, 1)
    correlate(owned, unit, lagged, block_of, correlation)
    stack_rows(correlation, lags, 0, rows_of(owned, block_of), away, scale)


def second_kernel(owned, scale, lagged, unit, lags, correlation, away):
    block_of = owners(away.shape[0] // owned, 0)
    correlate(owned, unit, lagged, block_of, correlation)
    stack_rows(correlation, lags, 0, rows_of(owned, block_of), away, scale)


def home_kernel(owned, scale, across, correlation, lags, target):
    rest = target.shape[0] // owned
    block_of = owners(rest, across)
    stack_rows(
        correlation, lags, target.shape[0], rows_of(owned, lambda b: block_of(b + rest)), target, scale
    )


def split_kernel(home, core, pair, own, *others):
    owned = own.shape[0]
    _, _, rest = place()
    for k, target in enumerate((own,) + others):
        at = pl.ds(pl.multiple_of((rest ^ k) * owned, 16), owned)
        total = home[at, :] + core[at, :].astype(f32) + pair[at, :].astype(f32)
        target[...] = total.astype(target.dtype)


def shards(records, templates, moveout, gap_start, gap_length):
    stations, _, width = records.shape
    number = templates.shape[0]
    full = width + MAXMO
    devices = lax.axis_size("tm")
    groups = lax.axis_size("sta")
    owned = number // groups
    rest = groups // 4
    scale = math.sqrt(TEMPLATE_LEN / (3.0 * stations * groups))
    own = records.transpose(1, 0, 2)
    following = lax.ppermute(own, "tm", [(i, (i - 1) % devices) for i in range(devices)])
    vmem = pl.BlockSpec(memory_space=pltpu.VMEM)
    hbm = pl.BlockSpec(memory_space=pltpu.HBM)
    depth = CHANNELS * PADDED

    def call(kernel, outs, ins, scratch=(), flops=10**9):
        return pl.pallas_call(
            kernel,
            out_shape=tuple(jax.ShapeDtypeStruct(shape, dtype) for shape, dtype in outs),
            in_specs=ins,
            out_specs=tuple(vmem for _ in outs),
            scratch_shapes=scratch,
            compiler_params=pltpu.CompilerParams(vmem_limit_bytes=24 * 1024 * 1024),
            cost_estimate=pl.CostEstimate(flops=flops, bytes_accessed=2 * 10**6, transcendentals=0),
        )

    flat = templates.transpose(2, 3, 1, 0).reshape(CHANNELS, TEMPLATE_LEN, stations, number // LANES, LANES)
    flat = flat.transpose(0, 1, 3, 2, 4).reshape(CHANNELS, TEMPLATE_LEN * stations * number // LANES, LANES)
    unit, lags, kept, masked = call(
        setup_kernel,
        [
            ((stations, number, depth), bf16),
            ((stations, number, LANES), i32),
            ((8, width), f32),
            ((8, width), f32),
        ],
        [hbm] * 5,
        [
            pltpu.VMEM((CHANNELS, TEMPLATE_LEN * stations * number // LANES, LANES), bf16),
            pltpu.VMEM((stations, number), i32),
            pltpu.SMEM((stations, CHANNELS), i32),
            pltpu.SMEM((stations, CHANNELS), i32),
            pltpu.VMEM((CHANNELS, stations, width), bf16),
            pltpu.VMEM((TEMPLATE_LEN * stations * number // LANES, LANES), f32),
            pltpu.VMEM((stations, number // LANES, depth, LANES), bf16),
            pltpu.VMEM((8, number), f32),
            pltpu.VMEM((8, width), f32),
            pltpu.SemaphoreType.DMA((CHANNELS + 4,)),
        ],
    )(
        *(
            pltpu.with_memory_space_constraint(a, pltpu.HBM)
            for a in (flat, moveout.T, gap_start, gap_length, own)
        )
    )
    half = ((stations, number // 2, full), f32)
    quarter = (number // 4, width)
    lagged, correlation, away = call(
        functools.partial(first_kernel, owned, scale),
        [((stations, depth, full), bf16), half, (quarter, bf16)],
        [vmem] * 5,
        [
            pltpu.VMEM((2 * width // LANES, 8 * STEP, LANES), f32),
            pltpu.VMEM((8, full), f32),
        ],
    )(masked, kept, following, unit, lags)

    def exchange(value, bit):
        return lax.ppermute(value, "sta", [(i, i ^ bit) for i in range(groups)])

    from_core = exchange(away, 1)
    (to_pair,) = call(functools.partial(home_kernel, owned, scale, 1), [(quarter, f32)], [vmem] * 2)(correlation, lags)
    to_pair = (to_pair + from_core.astype(f32)).astype(bf16)
    from_pair = exchange(to_pair, 2)
    correlation, away = call(
        functools.partial(second_kernel, owned, scale), [half, (quarter, bf16)], [vmem] * 3
    )(lagged, unit, lags)
    from_core = exchange(away, 1)
    (home,) = call(functools.partial(home_kernel, owned, scale, 0), [(quarter, f32)], [vmem] * 2)(correlation, lags)
    mine, *others = call(
        split_kernel, [((owned, width), f32)] + [((owned, width), bf16)] * (rest - 1), [vmem] * 3
    )(home, from_core, from_pair)
    arrived = [exchange(others[k - 1], 4 * k) for k in range(rest - 1, 0, -1)]
    for part in arrived:
        mine = mine + part.astype(f32)
    return mine


def solution(mesh):
    placed = (
        P("sta", None, "tm"),
        P(None, "sta", None, None),
        P(None, "sta"),
        P("sta", None),
        P("sta", None),
    )
    return jax.shard_map(
        shards, mesh=mesh, in_specs=placed, out_specs=P("sta", "tm"), check_vma=False
    )
```

time: 113 us -> 23.4 us (0.21)
  waiting for transfers between devices: 61.9 us -> 7.54 us
  local copies, waits for them, and re-layouts: 16.3 us -> 0 us
  other arithmetic: 15.4 us -> 0.67 us
  between operations: 13.9 us -> 0.08 us
  starting transfers between devices: 1.41 us -> 9.77 us
  Pallas kernels: 0 us -> 5.15 us
  matrix products: 3.41 us -> 0 us
    reduce_scatter x1 -> x0, waiting for transfers between devices: 60.4 us -> none  [shards(): lax.psum_scatter(lax.fori_loop(0, sta_dev, add_station, jnp.zeros((TEMPLA...]
    unnamed x162 -> x0, local copies, waits for them, and re-layouts: 14 us -> none
    ppermute x1 -> x7, starting transfers between devices: 1.41 us -> 9.77 us  [the longest x6 6.77 us: exchange(): return lax.ppermute(value, 'sta', [(i, i ^ bit) for i in range(groups)])]
    select_n x17 -> x0, other arithmetic: 6.79 us -> none  [the longest x16 6.7 us: shift_rows(): current = jnp.where(flagged, moved, kept)]
    ppermute x1 -> x7, waiting for transfers between devices: 1.46 us -> 7.54 us  [the longest x6 7.53 us: exchange(): return lax.ppermute(value, 'sta', [(i, i ^ bit) for i in range(groups)])]
    pallas_call x0 -> x6, Pallas kernels: none -> 5.15 us  [the longest x1 2.16 us: shards(): call(setup_kernel, [((stations, number, depth), bf16), ((stations, number...]
    reduce_sum x2 -> x0, other arithmetic: 3.64 us -> none  [the longest x1 2.15 us: unit_templates(): jnp.sum(widened * widened, axis=-1, keepdims=True) + 1e-06]
    dot_general x2 -> x0, matrix products: 3.41 us -> none  [add_station(): jnp.dot(weight_rows, station_data, preferred_element_type=jnp.float32)]
  transfers between devices with their start and end apart: 2 -> 7, of which waited for: 2 -> 3; matrix products, arithmetic and copies ran while one was open for 3% -> 0% of each run, Pallas kernels for 0% -> 16%
where the time goes in v2:
time: 23.4 us; the launch traced here: 23.2 us
  starting transfers between devices  9.77 us (42%)
  waiting for transfers between devices  7.54 us (32%)
  Pallas kernels  5.15 us (22%)
  other arithmetic  0.67 us (3%)
    ppermute x6, waiting for transfers between devices, exchange(): return lax.ppermute(value, 'sta', [(i, i ^ bit) for i in range(groups)])  7.53 us
    ppermute x6, starting transfers between devices, exchange(): return lax.ppermute(value, 'sta', [(i, i ^ bit) for i in range(groups)])  6.77 us
    ppermute x1, starting transfers between devices, shards(): lax.ppermute(own, 'tm', [(i, (i - 1) % devices) for i in range(devices)])  3 us
    pallas_call x1, Pallas kernels, shards(): call(setup_kernel, [((stations, number, depth), bf16), ((stations, number...  2.16 us
    pallas_call x1, Pallas kernels, shards(): call(functools.partial(first_kernel, owned, scale), [((stations, depth, f...  1.37 us
    pallas_call x1, Pallas kernels, shards(): call(functools.partial(second_kernel, owned, scale), [half, (quarter, bf1...  0.73 us
    add x1, other arithmetic, shards(): mine = mine + part.astype(f32)  0.65 us
  transfers between devices with their start and end apart: 7, of which 3 were waited for; matrix products, arithmetic and copies ran while one was open for 0% of the time, Pallas kernels for 16%

profile of v2, /device:TPU:0, one launch (start us, length us, event | category | flops | bytes accessed | tf_op | source)
XLA Modules:
  0.0 23.2 jit_solution(14762205659608525547)
XLA Ops:
  0.0 3.0 %collective-permute-start = (bf16[3,2,512]{2,1,0:T(2,128)(2,1)}, bf16[3,2,512]{2,1,0:T(2,128)(2,1)S(1)}, u32[]{:S(2)}, u32[]{:S(2)}) collective-permute-start(bf16[3,2,512]{2,1,0:T(2,128)(2,1)} %bitcast.10), channel_id=1, source_target_pairs={{0,1},{1,0},{2,3},{3,2},{4,5},{5,4},{6,7},{7,6},{8,9},{9,8},{10,11... | collective-permute-start | bytes 18440 | tf_op jit(solution)/shard_map/ppermute | solution.py:220
  3.0 2.2 %shard_map.55 = (bf16[2,512,480]{2,1,0:T(8,128)(2,1)S(1)}, s32[2,512,128]{2,1,0:T(8,128)S(1)}, f32[8,512]{1,0:T(8,128)S(1)}, f32[8,512]{1,0:T(8,128)S(1)}) custom-call(bf16[3,1200,128]{2,1,0:T(8,128)(2,1)} %bitcast.9, s32[2,512]{1,0:T(2,128)} %bitcast.12, s32[2,3]{1,0:T(2,128)} %gap_start_hbm.1, s32[2,3]{1,0:T(2,128)} %gap_length_hbm.1, ...), custom_call_target="tpu_custom_call" | custom-call | flops 1000000000 | bytes 2000000 | tf_op jit(solution)/shard_map/pallas_call | solution.py:238
  5.2 0.0 collective-permute-done.following
  5.2 1.4 %shard_map.56 = (bf16[2,480,768]{2,1,0:T(8,128)(2,1)S(1)}, f32[2,256,768]{2,1,0:T(8,128)S(1)}, bf16[128,512]{1,0:T(8,128)(2,1)S(1)}) custom-call(f32[8,512]{1,0:T(8,128)S(1)} %get-tuple-element.18.masked, f32[8,512]{1,0:T(8,128)S(1)} %get-tuple-element.19.kept, bf16[3,2,512]{2,1,0:T(2,128)(2,1)S(1)} %collective-permute-done.following, ...), custom_call_target="tpu_custom_call" | custom-call | flops 1000000000 | bytes 2000000 | tf_op jit(solution)/shard_map/pallas_call | solution.py:267
  6.5 0.1 collective-permute-start.2
  6.6 0.7 %shard_map.57 = (f32[2,256,768]{2,1,0:T(8,128)S(1)}, bf16[128,512]{1,0:T(8,128)(2,1)S(1)}) custom-call(bf16[2,480,768]{2,1,0:T(8,128)(2,1)S(1)} %get-tuple-element.22.lagged, bf16[2,512,480]{2,1,0:T(8,128)(2,1)S(1)} %get-tuple-element.20.unit, s32[2,512,128]{2,1,0:T(8,128)S(1)} %get-tuple-element.21.lags), custom_call_target="tpu_custom_call" | custom-call | flops 1000000000 | bytes 2000000 | tf_op jit(solution)/shard_map/pallas_call | solution.py:284
  7.4 0.6 %collective-permute-start.1 = (bf16[128,512]{1,0:T(8,128)(2,1)S(1)}, bf16[128,512]{1,0:T(8,128)(2,1)S(1)}, u32[]{:S(2)}, u32[]{:S(2)}) collective-permute-start(bf16[128,512]{1,0:T(8,128)(2,1)S(1)} %get-tuple-element.24), channel_id=1, source_target_pairs={{0,2},{2,0},{4,6},{6,4},{8,10},{10,8},{12,14},{14,12},{16,18},{18,... | collective-permute-start | bytes 393224 | tf_op jit(solution)/shard_map/ppermute | solution.py:278
  7.9 0.4 %shard_map.59 = f32[128,512]{1,0:T(8,128)S(1)} custom-call(f32[2,256,768]{2,1,0:T(8,128)S(1)} %get-tuple-element.25.correlation, s32[2,512,128]{2,1,0:T(8,128)S(1)} %get-tuple-element.21.lags), custom_call_target="tpu_custom_call" | custom-call | flops 1000000000 | bytes 2000000 | tf_op jit(solution)/shard_map/pallas_call | solution.py:281
  8.4 0.0 collective-permute-done.2
  8.4 1.7 %collective-permute-start.3 = (bf16[128,512]{1,0:T(8,128)(2,1)S(1)}, bf16[128,512]{1,0:T(8,128)(2,1)S(1)}, u32[]{:S(2)}, u32[]{:S(2)}) collective-permute-start(bf16[128,512]{1,0:T(8,128)(2,1)S(1)} %add_convert_fusion), channel_id=1, source_target_pairs={{0,4},{2,6},{4,0},{6,2},{8,12},{10,14},{12,8},{14,10},{16,20},{18,... | collective-permute-start | bytes 393224 | tf_op jit(solution)/shard_map/ppermute | solution.py:278
  10.1 0.4 %shard_map.58.home = f32[128,512]{1,0:T(8,128)S(1)} custom-call(f32[2,256,768]{2,1,0:T(8,128)S(1)} %get-tuple-element.23.correlation, s32[2,512,128]{2,1,0:T(8,128)S(1)} %get-tuple-element.21.lags), custom_call_target="tpu_custom_call" | custom-call | flops 1000000000 | bytes 2000000 | tf_op jit(solution)/shard_map/pallas_call | solution.py:288
  10.5 0.0 collective-permute-done.1.core
  10.5 3.4 %collective-permute-done.3.pair = bf16[128,512]{1,0:T(8,128)(2,1)S(1)} collective-permute-done((bf16[128,512]{1,0:T(8,128)(2,1)S(1)}, bf16[128,512]{1,0:T(8,128)(2,1)S(1)}, u32[]{:S(2)}, u32[]{:S(2)}) %collective-permute-start.3) | collective-permute-done | bytes 131104 | tf_op jit(solution)/shard_map/ppermute | solution.py:278
  13.9 3.8 %collective-permute-start.4 = (bf16[32,512]{1,0:T(8,128)(2,1)S(1)}, bf16[32,512]{1,0:T(8,128)(2,1)S(1)}, u32[]{:S(2)}, u32[]{:S(2)}) collective-permute-start(bf16[32,512]{1,0:T(8,128)(2,1)S(1)} %get-tuple-element.28), channel_id=1, source_target_pairs={{0,24},{2,26},{4,28},{6,30},{8,16},{10,18},{12,20},{14,22},{16,8},... | collective-permute-start | bytes 98312 | tf_op jit(solution)/shard_map/ppermute | solution.py:278
  17.7 0.0 collective-permute-start.5
  17.7 0.6 %collective-permute-start.6 = (bf16[32,512]{1,0:T(8,128)(2,1)S(1)}, bf16[32,512]{1,0:T(8,128)(2,1)S(1)}, u32[]{:S(2)}, u32[]{:S(2)}) collective-permute-start(bf16[32,512]{1,0:T(8,128)(2,1)S(1)} %get-tuple-element.30), channel_id=1, source_target_pairs={{0,8},{2,10},{4,12},{6,14},{8,0},{10,2},{12,4},{14,6},{16,24},{18,... | collective-permute-start | bytes 98312 | tf_op jit(solution)/shard_map/ppermute | solution.py:278
  18.4 1.5 %collective-permute-done.4 = bf16[32,512]{1,0:T(8,128)(2,1)S(1)} collective-permute-done((bf16[32,512]{1,0:T(8,128)(2,1)S(1)}, bf16[32,512]{1,0:T(8,128)(2,1)S(1)}, u32[]{:S(2)}, u32[]{:S(2)}) %collective-permute-start.4) | collective-permute-done | bytes 32800 | tf_op jit(solution)/shard_map/ppermute | solution.py:278
  19.9 2.6 %collective-permute-done.5 = bf16[32,512]{1,0:T(8,128)(2,1)S(1)} collective-permute-done((bf16[32,512]{1,0:T(8,128)(2,1)S(1)}, bf16[32,512]{1,0:T(8,128)(2,1)S(1)}, u32[]{:S(2)}, u32[]{:S(2)}) %collective-permute-start.5) | collective-permute-done | bytes 32800 | tf_op jit(solution)/shard_map/ppermute | solution.py:278
  22.6 0.0 collective-permute-done.6
  22.6 0.6 %convert_add_fusion = f32[32,512]{1,0:T(8,128)} fusion(bf16[32,512]{1,0:T(8,128)(2,1)S(1)} %collective-permute-done.6, bf16[32,512]{1,0:T(8,128)(2,1)S(1)} %collective-permute-done.5, f32[32,512]{1,0:T(8,128)S(1)} %get-tuple-element.27, bf16[32,512]{1,0:T(8,128)(2,1)S(1)} %collective-permute-done.4), kind=kLoop, calls=%fused_computation.1 | loop fusion | flops 98304 | bytes 229376 | tf_op jit(solution)/shard_map/add | solution.py:294
  (2 shorter events, 0.1 us)
Async XLA Ops:
  0.0 5.2 %collective-permute-start = (bf16[3,2,512]{2,1,0:T(2,128)(2,1)}, bf16[3,2,512]{2,1,0:T(2,128)(2,1)S(1)}, u32[]{:S(2)}, u32[]{:S(2)}) collective-permute-start(bf16[3,2,512]{2,1,0:T(2,128)(2,1)} %bitcast.10), channel_id=1, source_target_pairs={{0,1},{1,0},{2,3},{3,2},{4,5},{5,4},{6,7},{7,6},{8,9},{9,8},{10,11... | collective-permute-start | bytes 18440 | tf_op jit(solution)/shard_map/ppermute | solution.py:220
  6.5 1.8 %collective-permute-start.2 = (bf16[128,512]{1,0:T(8,128)(2,1)S(1)}, bf16[128,512]{1,0:T(8,128)(2,1)S(1)}, u32[]{:S(2)}, u32[]{:S(2)}) collective-permute-start(bf16[128,512]{1,0:T(8,128)(2,1)S(1)} %get-tuple-element.26), channel_id=1, source_target_pairs={{0,2},{2,0},{4,6},{6,4},{8,10},{10,8},{12,14},{14,12},{16,18},{18,... | collective-permute-start | bytes 393224 | tf_op jit(solution)/shard_map/ppermute | solution.py:278
  7.4 3.2 %collective-permute-start.1 = (bf16[128,512]{1,0:T(8,128)(2,1)S(1)}, bf16[128,512]{1,0:T(8,128)(2,1)S(1)}, u32[]{:S(2)}, u32[]{:S(2)}) collective-permute-start(bf16[128,512]{1,0:T(8,128)(2,1)S(1)} %get-tuple-element.24), channel_id=1, source_target_pairs={{0,2},{2,0},{4,6},{6,4},{8,10},{10,8},{12,14},{14,12},{16,18},{18,... | collective-permute-start | bytes 393224 | tf_op jit(solution)/shard_map/ppermute | solution.py:278
  8.4 5.5 %collective-permute-start.3 = (bf16[128,512]{1,0:T(8,128)(2,1)S(1)}, bf16[128,512]{1,0:T(8,128)(2,1)S(1)}, u32[]{:S(2)}, u32[]{:S(2)}) collective-permute-start(bf16[128,512]{1,0:T(8,128)(2,1)S(1)} %add_convert_fusion), channel_id=1, source_target_pairs={{0,4},{2,6},{4,0},{6,2},{8,12},{10,14},{12,8},{14,10},{16,20},{18,... | collective-permute-start | bytes 393224 | tf_op jit(solution)/shard_map/ppermute | solution.py:278
  13.9 6.0 %collective-permute-start.4 = (bf16[32,512]{1,0:T(8,128)(2,1)S(1)}, bf16[32,512]{1,0:T(8,128)(2,1)S(1)}, u32[]{:S(2)}, u32[]{:S(2)}) collective-permute-start(bf16[32,512]{1,0:T(8,128)(2,1)S(1)} %get-tuple-element.28), channel_id=1, source_target_pairs={{0,24},{2,26},{4,28},{6,30},{8,16},{10,18},{12,20},{14,22},{16,8},... | collective-permute-start | bytes 98312 | tf_op jit(solution)/shard_map/ppermute | solution.py:278
  17.7 4.8 %collective-permute-start.5 = (bf16[32,512]{1,0:T(8,128)(2,1)S(1)}, bf16[32,512]{1,0:T(8,128)(2,1)S(1)}, u32[]{:S(2)}, u32[]{:S(2)}) collective-permute-start(bf16[32,512]{1,0:T(8,128)(2,1)S(1)} %get-tuple-element.29), channel_id=1, source_target_pairs={{0,16},{2,18},{4,20},{6,22},{8,24},{10,26},{12,28},{14,30},{16,0},... | collective-permute-start | bytes 98312 | tf_op jit(solution)/shard_map/ppermute | solution.py:278
  17.7 4.8 %collective-permute-start.6 = (bf16[32,512]{1,0:T(8,128)(2,1)S(1)}, bf16[32,512]{1,0:T(8,128)(2,1)S(1)}, u32[]{:S(2)}, u32[]{:S(2)}) collective-permute-start(bf16[32,512]{1,0:T(8,128)(2,1)S(1)} %get-tuple-element.30), channel_id=1, source_target_pairs={{0,8},{2,10},{4,12},{6,14},{8,0},{10,2},{12,4},{14,6},{16,24},{18,... | collective-permute-start | bytes 98312 | tf_op jit(solution)/shard_map/ppermute | solution.py:278

commit v3 on v2

--- a/solution.py
+++ b/solution.py
@@ -34,12 +34,6 @@
         copy.start()
     for copy in small:
         copy.wait()
-    lag_rows[...] = jnp.zeros_like(lag_rows)
-    lag_rows[pl.ds(0, stations), :] = moveout[...].astype(f32)
-    for k in range(0, templates, LANES):
-        columns = lag_rows[:, pl.ds(k, LANES)].T
-        for s in range(stations):
-            lags[s, pl.ds(k, LANES), :] = jnp.broadcast_to(columns[:, s : s + 1], (LANES, LANES)).astype(i32)
     count = rows.shape[0]
     row = lax.broadcasted_iota(i32, (count, 1), 0)
     first = jnp.zeros((count, 1), i32)
@@ -55,16 +49,23 @@
     keep = ((position < first) | (position >= first + length)) & (position < lax.axis_size("tm") * width)
     kept[...] = jnp.where(keep[:, width:], 1.0, 0.0)
     masked[...] = jnp.where(keep[:, :width], rows[...], 0.0)
-    tall[...] = jnp.zeros_like(tall)
     groups = templates // LANES
     for c in range(CHANNELS):
         copies[c].wait()
+        if c == 0:
+            lag_rows[...] = jnp.zeros_like(lag_rows)
+            lag_rows[pl.ds(0, stations), :] = moveout[...].astype(f32)
+            for k in range(0, templates, LANES):
+                columns = lag_rows[:, pl.ds(k, LANES)].T
+                for s in range(stations):
+                    lags[s, pl.ds(k, LANES), :] = jnp.broadcast_to(columns[:, s : s + 1], (LANES, LANES)).astype(i32)
         apart[...] = raw[c].astype(f32)
         for j in range(groups):
             for s in range(stations):
                 wave = apart[pl.ds(j * stations + s, TEMPLATE_LEN, stride=groups * stations), :]
                 norm = lax.rsqrt(jnp.sum(wave * wave, axis=0, keepdims=True) + 1e-6)
-                tall[s, j, pl.ds(c * PADDED, TEMPLATE_LEN), :] = (wave * norm).astype(bf16)
+                wave = jnp.concatenate([wave * norm, jnp.zeros((PADDED - TEMPLATE_LEN, LANES), f32)], axis=0)
+                tall[s, j, pl.ds(c * PADDED, PADDED), :] = wave.astype(bf16)
     for s in range(stations):
         for j in range(templates // LANES):
             unit[s, pl.ds(j * LANES, LANES), :] = tall[s, j].T
@@ -170,40 +171,25 @@
         )
 
 
-def owners(rest, across):
-    core, pair, _ = place()
-    return lambda b: (b % rest * 2 + (pair ^ across)) * 2 + (core ^ 1 ^ (b // rest))
+def quarter_kernel(owned, scale, other_pair, other_core, lagged, unit, lags, target, correlation):
+    core, pair, rest = place()
+    block_of = lambda b: ((rest ^ b) * 2 + (pair ^ other_pair)) * 2 + (core ^ other_core)
+    correlate(owned, unit, lagged, block_of, correlation)
+    stack_rows(correlation, lags, 0, rows_of(owned, block_of), target, scale)
 
 
 def first_kernel(
-    owned, scale, masked, kept, following, unit, lags, lagged, correlation, away, staggered, inverse,
+    owned, scale, masked, kept, following, unit, lags, lagged, away, correlation, staggered, inverse,
 ):
     lag_matrix(masked, kept, following, staggered, inverse, lagged)
-    block_of = owners(away.shape[0] // owned, 1)
-    correlate(owned, unit, lagged, block_of, correlation)
-    stack_rows(correlation, lags, 0, rows_of(owned, block_of), away, scale)
-
-
-def second_kernel(owned, scale, lagged, unit, lags, correlation, away):
-    block_of = owners(away.shape[0] // owned, 0)
-    correlate(owned, unit, lagged, block_of, correlation)
-    stack_rows(correlation, lags, 0, rows_of(owned, block_of), away, scale)
-
-
-def home_kernel(owned, scale, across, correlation, lags, target):
-    rest = target.shape[0] // owned
-    block_of = owners(rest, across)
-    stack_rows(
-        correlation, lags, target.shape[0], rows_of(owned, lambda b: block_of(b + rest)), target, scale
-    )
-
-
-def split_kernel(home, core, pair, own, *others):
-    owned = own.shape[0]
-    _, _, rest = place()
-    for k, target in enumerate((own,) + others):
-        at = pl.ds(pl.multiple_of((rest ^ k) * owned, 16), owned)
-        total = home[at, :] + core[at, :].astype(f32) + pair[at, :].astype(f32)
+    quarter_kernel(owned, scale, 1, 1, lagged, unit, lags, away, correlation)
+
+
+def sum_kernel(first, home, core, pair, *targets):
+    for k, target in enumerate(targets):
+        owned = target.shape[0]
+        here, there = pl.ds((first + k) * owned, owned), pl.ds(k * owned, owned)
+        total = home[here, :] + core[here, :].astype(f32) + pair[there, :].astype(f32)
         target[...] = total.astype(target.dtype)
 
 
@@ -262,34 +248,40 @@
             for a in (flat, moveout.T, gap_start, gap_length, own)
         )
     )
-    half = ((stations, number // 2, full), f32)
     quarter = (number // 4, width)
-    lagged, correlation, away = call(
+    columns = pltpu.VMEM((stations, number // 4, full), f32)
+    lagged, away = call(
         functools.partial(first_kernel, owned, scale),
-        [((stations, depth, full), bf16), half, (quarter, bf16)],
+        [((stations, depth, full), bf16), (quarter, bf16)],
         [vmem] * 5,
-        [
-            pltpu.VMEM((2 * width // LANES, 8 * STEP, LANES), f32),
-            pltpu.VMEM((8, full), f32),
-        ],
+        [columns, pltpu.VMEM((2 * width // LANES, 8 * STEP, LANES), f32), pltpu.VMEM((8, full), f32)],
     )(masked, kept, following, unit, lags)
 
     def exchange(value, bit):
         return lax.ppermute(value, "sta", [(i, i ^ bit) for i in range(groups)])
 
+    def stacked(other_pair, other_core, dtype):
+        kernel = functools.partial(quarter_kernel, owned, scale, other_pair, other_core)
+        return call(kernel, [(quarter, dtype)], [vmem] * 3, [columns])(lagged, unit, lags)[0]
+
     from_core = exchange(away, 1)
-    (to_pair,) = call(functools.partial(home_kernel, owned, scale, 1), [(quarter, f32)], [vmem] * 2)(correlation, lags)
-    to_pair = (to_pair + from_core.astype(f32)).astype(bf16)
-    from_pair = exchange(to_pair, 2)
-    correlation, away = call(
-        functools.partial(second_kernel, owned, scale), [half, (quarter, bf16)], [vmem] * 3
-    )(lagged, unit, lags)
+    to_pair = stacked(1, 0, f32)
+    far = rest - 1
+    at = far * owned
+    from_far = exchange((to_pair[at:] + from_core[at:].astype(f32)).astype(bf16), 2)
+    from_near = exchange((to_pair[:at] + from_core[:at].astype(f32)).astype(bf16), 2)
+    away = stacked(0, 1, bf16)
     from_core = exchange(away, 1)
-    (home,) = call(functools.partial(home_kernel, owned, scale, 0), [(quarter, f32)], [vmem] * 2)(correlation, lags)
-    mine, *others = call(
-        split_kernel, [((owned, width), f32)] + [((owned, width), bf16)] * (rest - 1), [vmem] * 3
-    )(home, from_core, from_pair)
-    arrived = [exchange(others[k - 1], 4 * k) for k in range(rest - 1, 0, -1)]
+    home = stacked(0, 0, f32)
+    block = (owned, width)
+    fars = call(
+        functools.partial(sum_kernel, far), [(block, bf16)] * (rest - far), [vmem] * 3
+    )(home, from_core, from_far)
+    arrived = [exchange(fars[k - far], 4 * k) for k in range(rest - 1, far - 1, -1)]
+    mine, *nears = call(
+        functools.partial(sum_kernel, 0), [(block, f32)] + [(block, bf16)] * (far - 1), [vmem] * 3
+    )(home, from_core, from_near)
+    arrived += [exchange(nears[k - 1], 4 * k) for k in range(far - 1, 0, -1)]
     for part in arrived:
         mine = mine + part.astype(f32)
     return mine

time: 23.4 us -> 22.4 us (0.957)
  waiting for transfers between devices: 7.54 us -> 3.61 us
  starting transfers between devices: 9.77 us -> 12.5 us
  Pallas kernels: 5.15 us -> 5.4 us
    ppermute x6 -> x7, waiting for transfers between devices: 7.53 us -> 3.61 us  [exchange(): return lax.ppermute(value, 'sta', [(i, i ^ bit) for i in range(groups)])]
    ppermute x6 -> x7, starting transfers between devices: 6.77 us -> 9.46 us  [exchange(): return lax.ppermute(value, 'sta', [(i, i ^ bit) for i in range(groups)])]
    pallas_call x4 -> x5, Pallas kernels: 1.62 us -> 1.82 us  [the longest x3 1.77 us: stacked(): call(kernel, [(quarter, dtype)], [vmem] * 3, [columns])(lagged, unit, lags)]
  transfers between devices with their start and end apart: 7 -> 8, of which waited for: 3 -> 3; matrix products, arithmetic and copies ran while one was open for 0% -> 0% of each run, Pallas kernels for 16% -> 18%
where the time goes in v3:
time: 22.4 us; the launch traced here: 22.2 us
  starting transfers between devices  12.5 us (56%)
  Pallas kernels  5.4 us (24%)
  waiting for transfers between devices  3.61 us (16%)
  other arithmetic  0.68 us (3%)
    ppermute x7, starting transfers between devices, exchange(): return lax.ppermute(value, 'sta', [(i, i ^ bit) for i in range(groups)])  9.46 us
    ppermute x7, waiting for transfers between devices, exchange(): return lax.ppermute(value, 'sta', [(i, i ^ bit) for i in range(groups)])  3.61 us
    ppermute x1, starting transfers between devices, shards(): lax.ppermute(own, 'tm', [(i, (i - 1) % devices) for i in range(devices)])  3 us
    pallas_call x1, Pallas kernels, shards(): call(setup_kernel, [((stations, number, depth), bf16), ((stations, number...  2.12 us
    pallas_call x3, Pallas kernels, stacked(): call(kernel, [(quarter, dtype)], [vmem] * 3, [columns])(lagged, unit, lags)  1.77 us
    pallas_call x1, Pallas kernels, shards(): call(functools.partial(first_kernel, owned, scale), [((stations, depth, f...  1.46 us
    add x1, other arithmetic, shards(): mine = mine + part.astype(f32)  0.65 us
  transfers between devices with their start and end apart: 8, of which 3 were waited for; matrix products, arithmetic and copies ran while one was open for 0% of the time, Pallas kernels for 18%

profile of v3, /device:TPU:0, one launch (start us, length us, event | category | flops | bytes accessed | tf_op | source)
XLA Modules:
  0.0 22.2 jit_solution(7406302272073736404)
XLA Ops:
  0.0 3.0 %collective-permute-start = (bf16[3,2,512]{2,1,0:T(2,128)(2,1)}, bf16[3,2,512]{2,1,0:T(2,128)(2,1)S(1)}, u32[]{:S(2)}, u32[]{:S(2)}) collective-permute-start(bf16[3,2,512]{2,1,0:T(2,128)(2,1)} %bitcast.10), channel_id=1, source_target_pairs={{0,1},{1,0},{2,3},{3,2},{4,5},{5,4},{6,7},{7,6},{8,9},{9,8},{10,11... | collective-permute-start | bytes 18440 | tf_op jit(solution)/shard_map/ppermute | solution.py:206
  3.0 2.1 %shard_map.55 = (bf16[2,512,480]{2,1,0:T(8,128)(2,1)S(1)}, s32[2,512,128]{2,1,0:T(8,128)S(1)}, f32[8,512]{1,0:T(8,128)S(1)}, f32[8,512]{1,0:T(8,128)S(1)}) custom-call(bf16[3,1200,128]{2,1,0:T(8,128)(2,1)} %bitcast.9, s32[2,512]{1,0:T(2,128)} %bitcast.12, s32[2,3]{1,0:T(2,128)} %gap_start_hbm.1, s32[2,3]{1,0:T(2,128)} %gap_length_hbm.1, ...), custom_call_target="tpu_custom_call" | custom-call | flops 1000000000 | bytes 2000000 | tf_op jit(solution)/shard_map/pallas_call | solution.py:224
  5.1 0.0 collective-permute-done.following
  5.1 1.5 %shard_map.56 = (bf16[2,480,768]{2,1,0:T(8,128)(2,1)S(1)}, bf16[128,512]{1,0:T(8,128)(2,1)S(1)}) custom-call(f32[8,512]{1,0:T(8,128)S(1)} %get-tuple-element.14.masked, f32[8,512]{1,0:T(8,128)S(1)} %get-tuple-element.15.kept, bf16[3,2,512]{2,1,0:T(2,128)(2,1)S(1)} %collective-permute-done.following, bf16[2,512,480]{2,1,0:T(8,128)(2,1)S(1)} %get-tuple-element.16.unit, ...), custom_call_target="tpu_custom_call" | custom-call | flops 1000000000 | bytes 2000000 | tf_op jit(solution)/shard_map/pallas_call | solution.py:253
  6.6 0.1 collective-permute-start.2
  6.7 0.6 %shard_map.58 = bf16[128,512]{1,0:T(8,128)(2,1)S(1)} custom-call(bf16[2,480,768]{2,1,0:T(8,128)(2,1)S(1)} %get-tuple-element.18.lagged, bf16[2,512,480]{2,1,0:T(8,128)(2,1)S(1)} %get-tuple-element.16.unit, s32[2,512,128]{2,1,0:T(8,128)S(1)} %get-tuple-element.17.lags), custom_call_target="tpu_custom_call" | custom-call | flops 1000000000 | bytes 2000000 | tf_op jit(solution)/shard_map/pallas_call | solution.py:265
  7.3 0.6 %collective-permute-start.1 = (bf16[128,512]{1,0:T(8,128)(2,1)S(1)}, bf16[128,512]{1,0:T(8,128)(2,1)S(1)}, u32[]{:S(2)}, u32[]{:S(2)}) collective-permute-start(bf16[128,512]{1,0:T(8,128)(2,1)S(1)} %shard_map.58), channel_id=1, source_target_pairs={{0,2},{2,0},{4,6},{6,4},{8,10},{10,8},{12,14},{14,12},{16,18},{18,... | collective-permute-start | bytes 393224 | tf_op jit(solution)/shard_map/ppermute | solution.py:261
  7.8 0.6 %shard_map.59 = f32[128,512]{1,0:T(8,128)S(1)} custom-call(bf16[2,480,768]{2,1,0:T(8,128)(2,1)S(1)} %get-tuple-element.18.lagged, bf16[2,512,480]{2,1,0:T(8,128)(2,1)S(1)} %get-tuple-element.16.unit, s32[2,512,128]{2,1,0:T(8,128)S(1)} %get-tuple-element.17.lags), custom_call_target="tpu_custom_call" | custom-call | flops 1000000000 | bytes 2000000 | tf_op jit(solution)/shard_map/pallas_call | solution.py:265
  8.4 0.0 collective-permute-done.2
  8.5 1.7 %collective-permute-start.4 = (bf16[32,512]{1,0:T(8,128)(2,1)S(1)}, bf16[32,512]{1,0:T(8,128)(2,1)S(1)}, u32[]{:S(2)}, u32[]{:S(2)}) collective-permute-start(bf16[32,512]{1,0:T(8,128)(2,1)S(1)} %fusion.1), channel_id=1, source_target_pairs={{0,4},{2,6},{4,0},{6,2},{8,12},{10,14},{12,8},{14,10},{16,20},{18,... | collective-permute-start | bytes 98312 | tf_op jit(solution)/shard_map/ppermute | solution.py:261
  10.2 0.4 %collective-permute-start.3 = (bf16[96,512]{1,0:T(8,128)(2,1)S(1)}, bf16[96,512]{1,0:T(8,128)(2,1)S(1)}, u32[]{:S(2)}, u32[]{:S(2)}) collective-permute-start(bf16[96,512]{1,0:T(8,128)(2,1)S(1)} %fusion), channel_id=1, source_target_pairs={{0,4},{2,6},{4,0},{6,2},{8,12},{10,14},{12,8},{14,10},{16,20},{18,... | collective-permute-start | bytes 294920 | tf_op jit(solution)/shard_map/ppermute | solution.py:261
  10.6 0.6 %shard_map.57.home = f32[128,512]{1,0:T(8,128)S(1)} custom-call(bf16[2,480,768]{2,1,0:T(8,128)(2,1)S(1)} %get-tuple-element.18.lagged, bf16[2,512,480]{2,1,0:T(8,128)(2,1)S(1)} %get-tuple-element.16.unit, s32[2,512,128]{2,1,0:T(8,128)S(1)} %get-tuple-element.17.lags), custom_call_target="tpu_custom_call" | custom-call | flops 1000000000 | bytes 2000000 | tf_op jit(solution)/shard_map/pallas_call | solution.py:265
  11.2 0.0 collective-permute-done.1.core
  11.2 1.2 %collective-permute-done.4.pair = bf16[32,512]{1,0:T(8,128)(2,1)S(1)} collective-permute-done((bf16[32,512]{1,0:T(8,128)(2,1)S(1)}, bf16[32,512]{1,0:T(8,128)(2,1)S(1)}, u32[]{:S(2)}, u32[]{:S(2)}) %collective-permute-start.4) | collective-permute-done | bytes 32800 | tf_op jit(solution)/shard_map/ppermute | solution.py:261
  12.5 3.9 %collective-permute-start.5 = (bf16[32,512]{1,0:T(8,128)(2,1)S(1)}, bf16[32,512]{1,0:T(8,128)(2,1)S(1)}, u32[]{:S(2)}, u32[]{:S(2)}) collective-permute-start(bf16[32,512]{1,0:T(8,128)(2,1)S(1)} %shard_map.61), channel_id=1, source_target_pairs={{0,24},{2,26},{4,28},{6,30},{8,16},{10,18},{12,20},{14,22},{16,8},... | collective-permute-start | bytes 98312 | tf_op jit(solution)/shard_map/ppermute | solution.py:261
  16.3 0.0 collective-permute-done.3.pair
  16.4 1.2 %collective-permute-start.6 = (bf16[32,512]{1,0:T(8,128)(2,1)S(1)}, bf16[32,512]{1,0:T(8,128)(2,1)S(1)}, u32[]{:S(2)}, u32[]{:S(2)}) collective-permute-start(bf16[32,512]{1,0:T(8,128)(2,1)S(1)} %get-tuple-element.21), channel_id=1, source_target_pairs={{0,16},{2,18},{4,20},{6,22},{8,24},{10,26},{12,28},{14,30},{16,0},... | collective-permute-start | bytes 98312 | tf_op jit(solution)/shard_map/ppermute | solution.py:261
  17.6 1.6 %collective-permute-start.7 = (bf16[32,512]{1,0:T(8,128)(2,1)S(1)}, bf16[32,512]{1,0:T(8,128)(2,1)S(1)}, u32[]{:S(2)}, u32[]{:S(2)}) collective-permute-start(bf16[32,512]{1,0:T(8,128)(2,1)S(1)} %get-tuple-element.22), channel_id=1, source_target_pairs={{0,8},{2,10},{4,12},{6,14},{8,0},{10,2},{12,4},{14,6},{16,24},{18,... | collective-permute-start | bytes 98312 | tf_op jit(solution)/shard_map/ppermute | solution.py:261
  19.2 0.0 collective-permute-done.5
  19.2 2.1 %collective-permute-done.6 = bf16[32,512]{1,0:T(8,128)(2,1)S(1)} collective-permute-done((bf16[32,512]{1,0:T(8,128)(2,1)S(1)}, bf16[32,512]{1,0:T(8,128)(2,1)S(1)}, u32[]{:S(2)}, u32[]{:S(2)}) %collective-permute-start.6) | collective-permute-done | bytes 32800 | tf_op jit(solution)/shard_map/ppermute | solution.py:261
  21.2 0.3 %collective-permute-done.7 = bf16[32,512]{1,0:T(8,128)(2,1)S(1)} collective-permute-done((bf16[32,512]{1,0:T(8,128)(2,1)S(1)}, bf16[32,512]{1,0:T(8,128)(2,1)S(1)}, u32[]{:S(2)}, u32[]{:S(2)}) %collective-permute-start.7) | collective-permute-done | bytes 32800 | tf_op jit(solution)/shard_map/ppermute | solution.py:261
  21.6 0.6 %convert_add_fusion = f32[32,512]{1,0:T(8,128)} fusion(bf16[32,512]{1,0:T(8,128)(2,1)S(1)} %collective-permute-done.7, bf16[32,512]{1,0:T(8,128)(2,1)S(1)} %collective-permute-done.6, f32[32,512]{1,0:T(8,128)S(1)} %get-tuple-element.20, bf16[32,512]{1,0:T(8,128)(2,1)S(1)} %collective-permute-done.5), kind=kLoop, calls=%fused_computation.4 | loop fusion | flops 98304 | bytes 229376 | tf_op jit(solution)/shard_map/add | solution.py:286
  (4 shorter events, 0.1 us)
Async XLA Ops:
  0.0 5.1 %collective-permute-start = (bf16[3,2,512]{2,1,0:T(2,128)(2,1)}, bf16[3,2,512]{2,1,0:T(2,128)(2,1)S(1)}, u32[]{:S(2)}, u32[]{:S(2)}) collective-permute-start(bf16[3,2,512]{2,1,0:T(2,128)(2,1)} %bitcast.10), channel_id=1, source_target_pairs={{0,1},{1,0},{2,3},{3,2},{4,5},{5,4},{6,7},{7,6},{8,9},{9,8},{10,11... | collective-permute-start | bytes 18440 | tf_op jit(solution)/shard_map/ppermute | solution.py:206
  6.6 1.8 %collective-permute-start.2 = (bf16[128,512]{1,0:T(8,128)(2,1)S(1)}, bf16[128,512]{1,0:T(8,128)(2,1)S(1)}, u32[]{:S(2)}, u32[]{:S(2)}) collective-permute-start(bf16[128,512]{1,0:T(8,128)(2,1)S(1)} %get-tuple-element.19), channel_id=1, source_target_pairs={{0,2},{2,0},{4,6},{6,4},{8,10},{10,8},{12,14},{14,12},{16,18},{18,... | collective-permute-start | bytes 393224 | tf_op jit(solution)/shard_map/ppermute | solution.py:261
  7.3 4.0 %collective-permute-start.1 = (bf16[128,512]{1,0:T(8,128)(2,1)S(1)}, bf16[128,512]{1,0:T(8,128)(2,1)S(1)}, u32[]{:S(2)}, u32[]{:S(2)}) collective-permute-start(bf16[128,512]{1,0:T(8,128)(2,1)S(1)} %shard_map.58), channel_id=1, source_target_pairs={{0,2},{2,0},{4,6},{6,4},{8,10},{10,8},{12,14},{14,12},{16,18},{18,... | collective-permute-start | bytes 393224 | tf_op jit(solution)/shard_map/ppermute | solution.py:261
  8.5 4.0 %collective-permute-start.4 = (bf16[32,512]{1,0:T(8,128)(2,1)S(1)}, bf16[32,512]{1,0:T(8,128)(2,1)S(1)}, u32[]{:S(2)}, u32[]{:S(2)}) collective-permute-start(bf16[32,512]{1,0:T(8,128)(2,1)S(1)} %fusion.1), channel_id=1, source_target_pairs={{0,4},{2,6},{4,0},{6,2},{8,12},{10,14},{12,8},{14,10},{16,20},{18,... | collective-permute-start | bytes 98312 | tf_op jit(solution)/shard_map/ppermute | solution.py:261
  10.2 6.1 %collective-permute-start.3 = (bf16[96,512]{1,0:T(8,128)(2,1)S(1)}, bf16[96,512]{1,0:T(8,128)(2,1)S(1)}, u32[]{:S(2)}, u32[]{:S(2)}) collective-permute-start(bf16[96,512]{1,0:T(8,128)(2,1)S(1)} %fusion), channel_id=1, source_target_pairs={{0,4},{2,6},{4,0},{6,2},{8,12},{10,14},{12,8},{14,10},{16,20},{18,... | collective-permute-start | bytes 294920 | tf_op jit(solution)/shard_map/ppermute | solution.py:261
  12.5 6.7 %collective-permute-start.5 = (bf16[32,512]{1,0:T(8,128)(2,1)S(1)}, bf16[32,512]{1,0:T(8,128)(2,1)S(1)}, u32[]{:S(2)}, u32[]{:S(2)}) collective-permute-start(bf16[32,512]{1,0:T(8,128)(2,1)S(1)} %shard_map.61), channel_id=1, source_target_pairs={{0,24},{2,26},{4,28},{6,30},{8,16},{10,18},{12,20},{14,22},{16,8},... | collective-permute-start | bytes 98312 | tf_op jit(solution)/shard_map/ppermute | solution.py:261
  16.4 4.9 %collective-permute-start.6 = (bf16[32,512]{1,0:T(8,128)(2,1)S(1)}, bf16[32,512]{1,0:T(8,128)(2,1)S(1)}, u32[]{:S(2)}, u32[]{:S(2)}) collective-permute-start(bf16[32,512]{1,0:T(8,128)(2,1)S(1)} %get-tuple-element.21), channel_id=1, source_target_pairs={{0,16},{2,18},{4,20},{6,22},{8,24},{10,26},{12,28},{14,30},{16,0},... | collective-permute-start | bytes 98312 | tf_op jit(solution)/shard_map/ppermute | solution.py:261
  17.6 4.0 %collective-permute-start.7 = (bf16[32,512]{1,0:T(8,128)(2,1)S(1)}, bf16[32,512]{1,0:T(8,128)(2,1)S(1)}, u32[]{:S(2)}, u32[]{:S(2)}) collective-permute-start(bf16[32,512]{1,0:T(8,128)(2,1)S(1)} %get-tuple-element.22), channel_id=1, source_target_pairs={{0,8},{2,10},{4,12},{6,14},{8,0},{10,2},{12,4},{14,6},{16,24},{18,... | collective-permute-start | bytes 98312 | tf_op jit(solution)/shard_map/ppermute | solution.py:261

commit v4 on v3

--- a/solution.py
+++ b/solution.py
@@ -15,6 +15,7 @@
 LANES = 128
 PADDED = -(-TEMPLATE_LEN // 16) * 16
 
+PITCH = 17
 STEP = 16
 
 f32, bf16, i32 = jnp.float32, jnp.bfloat16, jnp.int32
@@ -89,13 +90,13 @@
     for r in range(STEP):
         moved = left(samples, r)
         for j in range(staggered.shape[0]):
-            staggered[j, pl.ds(r, count, stride=STEP), :] = moved[:, j * LANES : (j + 1) * LANES]
+            staggered[j, pl.ds(r, count, stride=PITCH), :] = moved[:, j * LANES : (j + 1) * LANES]
     lane = lax.broadcasted_iota(i32, (STEP, LANES), 1)
     for s in range(stations):
         for c in range(CHANNELS):
             r = c * stations + s
             tiles = [
-                staggered[j, pl.ds(STEP * r, STEP), :].astype(bf16) for j in range(staggered.shape[0])
+                staggered[j, pl.ds(PITCH * r, STEP), :].astype(bf16) for j in range(staggered.shape[0])
             ]
             scale = [
                 jnp.broadcast_to(inverse[pl.ds(r, 1), pl.ds(j * LANES, LANES)], (STEP, LANES))
@@ -254,7 +255,7 @@
         functools.partial(first_kernel, owned, scale),
         [((stations, depth, full), bf16), (quarter, bf16)],
         [vmem] * 5,
-        [columns, pltpu.VMEM((2 * width // LANES, 8 * STEP, LANES), f32), pltpu.VMEM((8, full), f32)],
+        [columns, pltpu.VMEM((2 * width // LANES, 8 * PITCH, LANES), f32), pltpu.VMEM((8, full), f32)],
     )(masked, kept, following, unit, lags)
 
     def exchange(value, bit):
@@ -265,14 +266,14 @@
         return call(kernel, [(quarter, dtype)], [vmem] * 3, [columns])(lagged, unit, lags)[0]
 
     from_core = exchange(away, 1)
+    away = stacked(0, 1, bf16)
     to_pair = stacked(1, 0, f32)
     far = rest - 1
     at = far * owned
     from_far = exchange((to_pair[at:] + from_core[at:].astype(f32)).astype(bf16), 2)
     from_near = exchange((to_pair[:at] + from_core[:at].astype(f32)).astype(bf16), 2)
-    away = stacked(0, 1, bf16)
+    home = stacked(0, 0, f32)
     from_core = exchange(away, 1)
-    home = stacked(0, 0, f32)
     block = (owned, width)
     fars = call(
         functools.partial(sum_kernel, far), [(block, bf16)] * (rest - far), [vmem] * 3

time: 22.4 us -> 22.3 us (level)
  no operation moved by 1% of the time
where the time goes in v4:
time: 22.3 us; the launch traced here: 22.2 us
  starting transfers between devices  12.5 us (56%)
  Pallas kernels  5.33 us (24%)
  waiting for transfers between devices  3.62 us (16%)
  other arithmetic  0.68 us (3%)
    ppermute x7, starting transfers between devices, exchange(): return lax.ppermute(value, 'sta', [(i, i ^ bit) for i in range(groups)])  9.46 us
    ppermute x7, waiting for transfers between devices, exchange(): return lax.ppermute(value, 'sta', [(i, i ^ bit) for i in range(groups)])  3.61 us
    ppermute x1, starting transfers between devices, shards(): lax.ppermute(own, 'tm', [(i, (i - 1) % devices) for i in range(devices)])  3 us
    pallas_call x1, Pallas kernels, shards(): call(setup_kernel, [((stations, number, depth), bf16), ((stations, number...  2.12 us
    pallas_call x3, Pallas kernels, stacked(): call(kernel, [(quarter, dtype)], [vmem] * 3, [columns])(lagged, unit, lags)  1.77 us
    pallas_call x1, Pallas kernels, shards(): call(functools.partial(first_kernel, owned, scale), [((stations, depth, f...  1.39 us
    add x1, other arithmetic, shards(): mine = mine + part.astype(f32)  0.65 us
  transfers between devices with their start and end apart: 8, of which 3 were waited for; matrix products, arithmetic and copies ran while one was open for 0% of the time, Pallas kernels for 18%

profile of v4, /device:TPU:0, one launch (start us, length us, event | category | flops | bytes accessed | tf_op | source)
XLA Modules:
  0.0 22.2 jit_solution(12113624900761717116)
XLA Ops:
  0.0 3.0 %collective-permute-start = (bf16[3,2,512]{2,1,0:T(2,128)(2,1)}, bf16[3,2,512]{2,1,0:T(2,128)(2,1)S(1)}, u32[]{:S(2)}, u32[]{:S(2)}) collective-permute-start(bf16[3,2,512]{2,1,0:T(2,128)(2,1)} %bitcast.10), channel_id=1, source_target_pairs={{0,1},{1,0},{2,3},{3,2},{4,5},{5,4},{6,7},{7,6},{8,9},{9,8},{10,11... | collective-permute-start | bytes 18440 | tf_op jit(solution)/shard_map/ppermute | solution.py:207
  3.0 2.1 %shard_map.55 = (bf16[2,512,480]{2,1,0:T(8,128)(2,1)S(1)}, s32[2,512,128]{2,1,0:T(8,128)S(1)}, f32[8,512]{1,0:T(8,128)S(1)}, f32[8,512]{1,0:T(8,128)S(1)}) custom-call(bf16[3,1200,128]{2,1,0:T(8,128)(2,1)} %bitcast.9, s32[2,512]{1,0:T(2,128)} %bitcast.12, s32[2,3]{1,0:T(2,128)} %gap_start_hbm.1, s32[2,3]{1,0:T(2,128)} %gap_length_hbm.1, ...), custom_call_target="tpu_custom_call" | custom-call | flops 1000000000 | bytes 2000000 | tf_op jit(solution)/shard_map/pallas_call | solution.py:225
  5.1 0.0 collective-permute-done.following
  5.1 1.4 %shard_map.56 = (bf16[2,480,768]{2,1,0:T(8,128)(2,1)S(1)}, bf16[128,512]{1,0:T(8,128)(2,1)S(1)}) custom-call(f32[8,512]{1,0:T(8,128)S(1)} %get-tuple-element.14.masked, f32[8,512]{1,0:T(8,128)S(1)} %get-tuple-element.15.kept, bf16[3,2,512]{2,1,0:T(2,128)(2,1)S(1)} %collective-permute-done.following, bf16[2,512,480]{2,1,0:T(8,128)(2,1)S(1)} %get-tuple-element.16.unit, ...), custom_call_target="tpu_custom_call" | custom-call | flops 1000000000 | bytes 2000000 | tf_op jit(solution)/shard_map/pallas_call | solution.py:254
  6.5 0.1 collective-permute-start.2
  6.6 0.6 %shard_map.58 = bf16[128,512]{1,0:T(8,128)(2,1)S(1)} custom-call(bf16[2,480,768]{2,1,0:T(8,128)(2,1)S(1)} %get-tuple-element.18.lagged, bf16[2,512,480]{2,1,0:T(8,128)(2,1)S(1)} %get-tuple-element.16.unit, s32[2,512,128]{2,1,0:T(8,128)S(1)} %get-tuple-element.17.lags), custom_call_target="tpu_custom_call" | custom-call | flops 1000000000 | bytes 2000000 | tf_op jit(solution)/shard_map/pallas_call | solution.py:266
  7.2 0.6 %collective-permute-start.1 = (bf16[128,512]{1,0:T(8,128)(2,1)S(1)}, bf16[128,512]{1,0:T(8,128)(2,1)S(1)}, u32[]{:S(2)}, u32[]{:S(2)}) collective-permute-start(bf16[128,512]{1,0:T(8,128)(2,1)S(1)} %shard_map.58), channel_id=1, source_target_pairs={{0,2},{2,0},{4,6},{6,4},{8,10},{10,8},{12,14},{14,12},{16,18},{18,... | collective-permute-start | bytes 393224 | tf_op jit(solution)/shard_map/ppermute | solution.py:262
  7.8 0.6 %shard_map.59 = f32[128,512]{1,0:T(8,128)S(1)} custom-call(bf16[2,480,768]{2,1,0:T(8,128)(2,1)S(1)} %get-tuple-element.18.lagged, bf16[2,512,480]{2,1,0:T(8,128)(2,1)S(1)} %get-tuple-element.16.unit, s32[2,512,128]{2,1,0:T(8,128)S(1)} %get-tuple-element.17.lags), custom_call_target="tpu_custom_call" | custom-call | flops 1000000000 | bytes 2000000 | tf_op jit(solution)/shard_map/pallas_call | solution.py:266
  8.4 0.0 collective-permute-done.2
  8.4 1.7 %collective-permute-start.4 = (bf16[32,512]{1,0:T(8,128)(2,1)S(1)}, bf16[32,512]{1,0:T(8,128)(2,1)S(1)}, u32[]{:S(2)}, u32[]{:S(2)}) collective-permute-start(bf16[32,512]{1,0:T(8,128)(2,1)S(1)} %fusion.1), channel_id=1, source_target_pairs={{0,4},{2,6},{4,0},{6,2},{8,12},{10,14},{12,8},{14,10},{16,20},{18,... | collective-permute-start | bytes 98312 | tf_op jit(solution)/shard_map/ppermute | solution.py:262
  10.2 0.4 %collective-permute-start.3 = (bf16[96,512]{1,0:T(8,128)(2,1)S(1)}, bf16[96,512]{1,0:T(8,128)(2,1)S(1)}, u32[]{:S(2)}, u32[]{:S(2)}) collective-permute-start(bf16[96,512]{1,0:T(8,128)(2,1)S(1)} %fusion), channel_id=1, source_target_pairs={{0,4},{2,6},{4,0},{6,2},{8,12},{10,14},{12,8},{14,10},{16,20},{18,... | collective-permute-start | bytes 294920 | tf_op jit(solution)/shard_map/ppermute | solution.py:262
  10.6 0.6 %shard_map.57.home = f32[128,512]{1,0:T(8,128)S(1)} custom-call(bf16[2,480,768]{2,1,0:T(8,128)(2,1)S(1)} %get-tuple-element.18.lagged, bf16[2,512,480]{2,1,0:T(8,128)(2,1)S(1)} %get-tuple-element.16.unit, s32[2,512,128]{2,1,0:T(8,128)S(1)} %get-tuple-element.17.lags), custom_call_target="tpu_custom_call" | custom-call | flops 1000000000 | bytes 2000000 | tf_op jit(solution)/shard_map/pallas_call | solution.py:266
  11.2 0.0 collective-permute-done.1.core
  11.2 1.2 %collective-permute-done.4.pair = bf16[32,512]{1,0:T(8,128)(2,1)S(1)} collective-permute-done((bf16[32,512]{1,0:T(8,128)(2,1)S(1)}, bf16[32,512]{1,0:T(8,128)(2,1)S(1)}, u32[]{:S(2)}, u32[]{:S(2)}) %collective-permute-start.4) | collective-permute-done | bytes 32800 | tf_op jit(solution)/shard_map/ppermute | solution.py:262
  12.4 3.9 %collective-permute-start.5 = (bf16[32,512]{1,0:T(8,128)(2,1)S(1)}, bf16[32,512]{1,0:T(8,128)(2,1)S(1)}, u32[]{:S(2)}, u32[]{:S(2)}) collective-permute-start(bf16[32,512]{1,0:T(8,128)(2,1)S(1)} %shard_map.61), channel_id=1, source_target_pairs={{0,24},{2,26},{4,28},{6,30},{8,16},{10,18},{12,20},{14,22},{16,8},... | collective-permute-start | bytes 98312 | tf_op jit(solution)/shard_map/ppermute | solution.py:262
  16.2 0.0 collective-permute-done.3.pair
  16.3 1.2 %collective-permute-start.6 = (bf16[32,512]{1,0:T(8,128)(2,1)S(1)}, bf16[32,512]{1,0:T(8,128)(2,1)S(1)}, u32[]{:S(2)}, u32[]{:S(2)}) collective-permute-start(bf16[32,512]{1,0:T(8,128)(2,1)S(1)} %get-tuple-element.21), channel_id=1, source_target_pairs={{0,16},{2,18},{4,20},{6,22},{8,24},{10,26},{12,28},{14,30},{16,0},... | collective-permute-start | bytes 98312 | tf_op jit(solution)/shard_map/ppermute | solution.py:262
  17.5 1.6 %collective-permute-start.7 = (bf16[32,512]{1,0:T(8,128)(2,1)S(1)}, bf16[32,512]{1,0:T(8,128)(2,1)S(1)}, u32[]{:S(2)}, u32[]{:S(2)}) collective-permute-start(bf16[32,512]{1,0:T(8,128)(2,1)S(1)} %get-tuple-element.22), channel_id=1, source_target_pairs={{0,8},{2,10},{4,12},{6,14},{8,0},{10,2},{12,4},{14,6},{16,24},{18,... | collective-permute-start | bytes 98312 | tf_op jit(solution)/shard_map/ppermute | solution.py:262
  19.1 0.0 collective-permute-done.5
  19.1 2.1 %collective-permute-done.6 = bf16[32,512]{1,0:T(8,128)(2,1)S(1)} collective-permute-done((bf16[32,512]{1,0:T(8,128)(2,1)S(1)}, bf16[32,512]{1,0:T(8,128)(2,1)S(1)}, u32[]{:S(2)}, u32[]{:S(2)}) %collective-permute-start.6) | collective-permute-done | bytes 32800 | tf_op jit(solution)/shard_map/ppermute | solution.py:262
  21.2 0.3 %collective-permute-done.7 = bf16[32,512]{1,0:T(8,128)(2,1)S(1)} collective-permute-done((bf16[32,512]{1,0:T(8,128)(2,1)S(1)}, bf16[32,512]{1,0:T(8,128)(2,1)S(1)}, u32[]{:S(2)}, u32[]{:S(2)}) %collective-permute-start.7) | collective-permute-done | bytes 32800 | tf_op jit(solution)/shard_map/ppermute | solution.py:262
  21.5 0.6 %convert_add_fusion = f32[32,512]{1,0:T(8,128)} fusion(bf16[32,512]{1,0:T(8,128)(2,1)S(1)} %collective-permute-done.7, bf16[32,512]{1,0:T(8,128)(2,1)S(1)} %collective-permute-done.6, f32[32,512]{1,0:T(8,128)S(1)} %get-tuple-element.20, bf16[32,512]{1,0:T(8,128)(2,1)S(1)} %collective-permute-done.5), kind=kLoop, calls=%fused_computation.4 | loop fusion | flops 98304 | bytes 229376 | tf_op jit(solution)/shard_map/add | solution.py:287
  (4 shorter events, 0.1 us)
Async XLA Ops:
  0.0 5.1 %collective-permute-start = (bf16[3,2,512]{2,1,0:T(2,128)(2,1)}, bf16[3,2,512]{2,1,0:T(2,128)(2,1)S(1)}, u32[]{:S(2)}, u32[]{:S(2)}) collective-permute-start(bf16[3,2,512]{2,1,0:T(2,128)(2,1)} %bitcast.10), channel_id=1, source_target_pairs={{0,1},{1,0},{2,3},{3,2},{4,5},{5,4},{6,7},{7,6},{8,9},{9,8},{10,11... | collective-permute-start | bytes 18440 | tf_op jit(solution)/shard_map/ppermute | solution.py:207
  6.5 1.8 %collective-permute-start.2 = (bf16[128,512]{1,0:T(8,128)(2,1)S(1)}, bf16[128,512]{1,0:T(8,128)(2,1)S(1)}, u32[]{:S(2)}, u32[]{:S(2)}) collective-permute-start(bf16[128,512]{1,0:T(8,128)(2,1)S(1)} %get-tuple-element.19), channel_id=1, source_target_pairs={{0,2},{2,0},{4,6},{6,4},{8,10},{10,8},{12,14},{14,12},{16,18},{18,... | collective-permute-start | bytes 393224 | tf_op jit(solution)/shard_map/ppermute | solution.py:262
  7.2 4.0 %collective-permute-start.1 = (bf16[128,512]{1,0:T(8,128)(2,1)S(1)}, bf16[128,512]{1,0:T(8,128)(2,1)S(1)}, u32[]{:S(2)}, u32[]{:S(2)}) collective-permute-start(bf16[128,512]{1,0:T(8,128)(2,1)S(1)} %shard_map.58), channel_id=1, source_target_pairs={{0,2},{2,0},{4,6},{6,4},{8,10},{10,8},{12,14},{14,12},{16,18},{18,... | collective-permute-start | bytes 393224 | tf_op jit(solution)/shard_map/ppermute | solution.py:262
  8.4 4.0 %collective-permute-start.4 = (bf16[32,512]{1,0:T(8,128)(2,1)S(1)}, bf16[32,512]{1,0:T(8,128)(2,1)S(1)}, u32[]{:S(2)}, u32[]{:S(2)}) collective-permute-start(bf16[32,512]{1,0:T(8,128)(2,1)S(1)} %fusion.1), channel_id=1, source_target_pairs={{0,4},{2,6},{4,0},{6,2},{8,12},{10,14},{12,8},{14,10},{16,20},{18,... | collective-permute-start | bytes 98312 | tf_op jit(solution)/shard_map/ppermute | solution.py:262
  10.2 6.1 %collective-permute-start.3 = (bf16[96,512]{1,0:T(8,128)(2,1)S(1)}, bf16[96,512]{1,0:T(8,128)(2,1)S(1)}, u32[]{:S(2)}, u32[]{:S(2)}) collective-permute-start(bf16[96,512]{1,0:T(8,128)(2,1)S(1)} %fusion), channel_id=1, source_target_pairs={{0,4},{2,6},{4,0},{6,2},{8,12},{10,14},{12,8},{14,10},{16,20},{18,... | collective-permute-start | bytes 294920 | tf_op jit(solution)/shard_map/ppermute | solution.py:262
  12.4 6.7 %collective-permute-start.5 = (bf16[32,512]{1,0:T(8,128)(2,1)S(1)}, bf16[32,512]{1,0:T(8,128)(2,1)S(1)}, u32[]{:S(2)}, u32[]{:S(2)}) collective-permute-start(bf16[32,512]{1,0:T(8,128)(2,1)S(1)} %shard_map.61), channel_id=1, source_target_pairs={{0,24},{2,26},{4,28},{6,30},{8,16},{10,18},{12,20},{14,22},{16,8},... | collective-permute-start | bytes 98312 | tf_op jit(solution)/shard_map/ppermute | solution.py:262
  16.3 4.9 %collective-permute-start.6 = (bf16[32,512]{1,0:T(8,128)(2,1)S(1)}, bf16[32,512]{1,0:T(8,128)(2,1)S(1)}, u32[]{:S(2)}, u32[]{:S(2)}) collective-permute-start(bf16[32,512]{1,0:T(8,128)(2,1)S(1)} %get-tuple-element.21), channel_id=1, source_target_pairs={{0,16},{2,18},{4,20},{6,22},{8,24},{10,26},{12,28},{14,30},{16,0},... | collective-permute-start | bytes 98312 | tf_op jit(solution)/shard_map/ppermute | solution.py:262
  17.5 4.0 %collective-permute-start.7 = (bf16[32,512]{1,0:T(8,128)(2,1)S(1)}, bf16[32,512]{1,0:T(8,128)(2,1)S(1)}, u32[]{:S(2)}, u32[]{:S(2)}) collective-permute-start(bf16[32,512]{1,0:T(8,128)(2,1)S(1)} %get-tuple-element.22), channel_id=1, source_target_pairs={{0,8},{2,10},{4,12},{6,14},{8,0},{10,2},{12,4},{14,6},{16,24},{18,... | collective-permute-start | bytes 98312 | tf_op jit(solution)/shard_map/ppermute | solution.py:262
